TPU v7x, 32 devices: a whole 2x2x4 slice. The times are simulated.
32 devices in a mesh: seq: 8 (over z, x), row: 2 (over core), col: 2 (over y).
Axes of the slice: x: 2, y: 2, z: 4, core: 2. Of those that a mesh axis runs over, the one named last changes fastest.
Arguments:
- tokens: bfloat16 [4096, 6144], P('seq', ('row', 'col')), may hold values from -20 to 20
- ln_gain: bfloat16 [6144], P(('row', 'col')), may hold values from 0.099609375 to 1.8984375
- ln_bias: bfloat16 [6144], P(('row', 'col')), may hold values from -1.5 to 1.5
- w_qkv: bfloat16 [3, 6144, 4096], P(None, 'row', 'col'), may hold values from -3 to 3
- w_out: bfloat16 [4096, 6144], P('col', 'row'), may hold values from -0.5 to 0.5
Outputs:
- attended: bfloat16 [4096, 6144], P('seq', ('row', 'col'))
All inputs are finite; a program needn't handle non-finite values.
Results may differ from a plain program's by a relative error of at most 0.014.
Values may be sent and summed in bfloat16 or wider, within the bound.
A program may use at most 192 MiB of HBM per device.

v0:
```python
import math

import jax
import jax.numpy as jnp
from jax import lax
from jax.sharding import PartitionSpec as P

D = 6144
HD = 128


EPS = 0.25


def block_length(row_total):
    block_size = row_total
    while block_size > 2048 and block_size % 2 == 0:
        block_size = block_size // 2
    return block_size


def initial_state(head_count, query_count):
    return (
        jnp.full((head_count, query_count), -1e30, jnp.float32),
        jnp.zeros((head_count, query_count), jnp.float32),
        jnp.zeros((head_count, query_count, HD), jnp.float32),
    )


def attend(carried, queries, key_rows, value_rows):
    score_scale = 1.0 / math.sqrt(HD)
    key_axis = 1
    row_total = key_rows.shape[key_axis]
    block_size = block_length(row_total)
    block_count = row_total // block_size
    key_form = "hkd"

    def fold_block(running, block_index):
        running_max, running_sum, weighted = running
        first = block_index * block_size
        key_block = lax.dynamic_slice_in_dim(key_rows, first, block_size, key_axis)
        value_block = lax.dynamic_slice_in_dim(value_rows, first, block_size, key_axis)
        scores = (
            jnp.einsum(
                "hqd," + key_form + "->hqk", queries, key_block, preferred_element_type=jnp.float32
            )
            * score_scale
        )
        new_max = jnp.maximum(running_max, jnp.max(scores, axis=2))
        shrink = jnp.exp(running_max - new_max)
        weights = jnp.exp(scores - new_max[:, :, None])
        running_sum = running_sum * shrink + jnp.sum(weights, axis=2)
        weighted = weighted * shrink[:, :, None] + jnp.einsum(
            "hqk," + key_form + "->hqd",
            weights.astype(jnp.bfloat16),
            value_block,
            preferred_element_type=jnp.float32,
        )
        return ((new_max, running_sum, weighted), None)

    folded, _ = lax.scan(fold_block, carried, jnp.arange(block_count, dtype=jnp.int32))
    return folded


def normalize_heads(folded):
    return (folded[2] / folded[1][:, :, None]).astype(jnp.bfloat16)


def flatten_heads(per_head):
    return jnp.transpose(per_head, (1, 0, 2)).reshape(per_head.shape[1], per_head.shape[0] * HD)


def body(tokens, ln_gain, ln_bias, w_qkv, w_out):
    seq_rows = tokens.shape[0]
    gain_row = ln_gain[None, :]
    bias_row = ln_bias[None, :]
    half_tok, half_gain, half_bias = (
        lax.all_gather(tokens, "col", axis=1, tiled=True),
        lax.all_gather(gain_row, "col", axis=1, tiled=True),
        lax.all_gather(bias_row, "col", axis=1, tiled=True),
    )
    as_float = half_tok.astype(jnp.float32)
    feature_sum, squares = lax.psum(
        (jnp.sum(as_float, axis=1), jnp.sum(as_float * as_float, axis=1)), "row"
    )
    token_mean = feature_sum / D
    spread = squares / D - token_mean * token_mean
    normed = (
        (as_float - token_mean[:, None])
        * lax.rsqrt(spread + EPS)[:, None]
        * half_gain.astype(jnp.float32)
        + half_bias.astype(jnp.float32)
    ).astype(jnp.bfloat16)
    local_heads = w_qkv.shape[2] // HD
    head_share = local_heads // lax.axis_size("row")
    columns = w_qkv
    columns = columns.reshape(3, columns.shape[1], lax.axis_size("row") * head_share, HD)
    owned = lax.psum_scatter(
        jnp.einsum("td,kdhe->hkte", normed, columns, preferred_element_type=jnp.float32),
        "row",
        scatter_dimension=0,
        tiled=True,
    ).astype(jnp.bfloat16)
    queries = owned[:, 0]
    folded = attend(
        initial_state(head_share, seq_rows),
        queries,
        lax.all_gather(owned[:, 1], "seq", axis=1, tiled=True),
        lax.all_gather(owned[:, 2], "seq", axis=1, tiled=True),
    )
    context = flatten_heads(normalize_heads(folded))
    partial_output = jnp.dot(
        lax.all_gather(context, "row", axis=1, tiled=True),
        w_out,
        preferred_element_type=jnp.float32,
    )
    summed_output = lax.psum_scatter(
        partial_output.astype(jnp.bfloat16), "col", scatter_dimension=1, tiled=True
    ).astype(jnp.float32)
    return (tokens.astype(jnp.float32) + summed_output).astype(jnp.bfloat16)


def solution(mesh):
    return jax.shard_map(
        body,
        mesh=mesh,
        in_specs=(
            P("seq", ("row", "col")),
            P(("row", "col")),
            P(("row", "col")),
            P(None, "row", "col"),
            P("col", "row"),
        ),
        out_specs=P("seq", ("row", "col")),
        check_vma=False,
    )
```

profile of v0, /device:TPU:0, one launch (start us, length us, event | category | flops | bytes accessed | tf_op | source)
XLA Modules:
  0.0 565.4 jit_solution(7507086611371644992)
XLA Ops:
  6.5 0.0 all-gather.11.cloned.1.call-start
  6.5 0.7 all-gather.11.cloned.1.call-update
  7.3 0.0 reduce-scatter.8.cloned.1.call-start
  7.3 0.7 reshape.25
  8.0 5.3 all-gather.4
  13.3 0.7 reshape.27
  14.0 4.4 all-gather.5
  18.4 38.1 %all-gather.11.cloned.1.call-done = bf16[512,3072]{1,0:T(8,128)(2,1)} async-done(((bf16[512,1536]{1,0:T(8,128)(2,1)}), bf16[512,3072]{1,0:T(8,128)(2,1)}) %all-gather.11.cloned.1.call-update) | async-done | bytes 3145744 | tf_op jit(solution)/shard_map/all_gather | solution.py:78
  56.5 2.9 convert_reduce_fusion
  59.4 2.5 all-reduce
  61.9 27.6 %fusion.27 = f32[16,3,512,128]{3,2,0,1:T(8,128)} fusion(bf16[512,3072]{1,0:T(8,128)(2,1)} %all-gather.11.cloned.1.call-done, f32[3072]{0:T(1024)S(1)} %bitcast.69, f32[3072]{0:T(1024)S(1)} %bitcast.68, f32[512]{0:T(512)S(1)} %get-tuple-element.105, f32[512]{0:T(512)S(1)} %get-tuple-element.104, bf16[3,3072,2048]{2,1,0:T(8,128)(2,1)} %param.10), kind=kOutput, calls=%fused_computation.34 | convolution fusion | flops 19336790016 | bytes 53506048 | tf_op jit(solution)/shard_map/td,kdhe->hkte/dot_general | solution.py:99
  89.5 10.5 %copy.16 = f32[16,3,512,128]{3,2,1,0:T(8,128)} copy(f32[16,3,512,128]{3,2,0,1:T(8,128)} %fusion.27) | data formatting | bytes 25165824
  100.0 14.3 %copy.32 = f32[2,8,1536,128]{3,1,2,0:T(8,128)} copy(f32[2,8,1536,128]{3,2,1,0:T(8,128)} %bitcast.64) | data formatting | bytes 25165824
  114.3 0.0 reduce-scatter.8.cloned.1.call-update
  114.4 0.2 all-gather.17.cloned.1.call-start
  114.6 20.7 %reduce-scatter.8.cloned.1.call-done = f32[8,196608]{1,0:T(8,128)} async-done(((f32[16,196608]{1,0:T(8,128)}), f32[8,196608]{1,0:T(8,128)}) %reduce-scatter.8.cloned.1.call-update) | async-done | bytes 6291472
  135.3 4.0 copy.20
  139.3 1.5 fusion.36
  140.8 0.0 all-gather.17.cloned.1.call-update
  140.8 0.0 all-gather.15.cloned.1.call-start
  140.8 0.5 all-gather.15.cloned.1.call-update
  141.4 0.0 all-gather.13.cloned.1.call-start
  141.5 126.3 %all-gather.17.cloned.1.call-done = bf16[8,1,4096,128]{3,2,0,1:T(8,128)(2,1)} async-done(((bf16[8,1,512,128]{3,2,0,1:T(8,128)(2,1)}), bf16[8,1,4096,128]{3,2,0,1:T(8,128)(2,1)}) %all-gather.17.cloned.1.call-update) | async-done | bytes 8388624 | tf_op jit(solution)/shard_map/all_gather | solution.py:109
  267.8 124.7 %all-gather.15.cloned.1.call-done = bf16[8,1,4096,128]{3,2,0,1:T(8,128)(2,1)} async-done(((bf16[8,1,512,128]{3,2,0,1:T(8,128)(2,1)}), bf16[8,1,4096,128]{3,2,0,1:T(8,128)(2,1)}) %all-gather.15.cloned.1.call-update) | async-done | bytes 8388624 | tf_op jit(solution)/shard_map/all_gather | solution.py:108
  392.5 91.8 %while.15 = (s32[]{:T(128)}, f32[8,512]{1,0:T(8,128)S(1)}, f32[8,512]{1,0:T(8,128)S(1)}, f32[8,512,128]{2,1,0:T(8,128)S(1)}, s32[2]{0:T(128)S(1)}, /*index=5*/bf...) while((s32[]{:T(128)}, f32[8,512]{1,0:T(8,128)S(1)}, ...), condition=%wide.region_8.9_spmd.clone, body=%wide.region_5.8_spmd.clone.sunk | while | flops 4363669504 | bytes 114557128 | solution.py:61
  392.5 0.6 dynamic_slice.26
  393.7 15.5 %bitcast_reduce_fusion.2 = (f32[8,512]{1,0:T(8,128)S(1)}, f32[8,2048,512]{2,1,0:T(8,128)}) fusion(bf16[8,512,128]{2,1,0:T(8,128)(2,1)S(1)} %get-tuple-element.193, bf16[8,4096,128]{2,1,0:T(8,128)(2,1)} %get-tuple-element.192, s32[]{:T(128)S(6)} %select_n.6), kind=kOutput, calls=%fused_computation.1.clone.1 | convolution fusion | flops 2164256768 | bytes 38813700 | tf_op jit(solution)/shard_map/while/body/eval_jaxpr/hqd,hkd->hqk/dot_general | solution.py:44
  409.2 13.6 %fusion.51 = f32[8,512]{1,0:T(8,128)S(1)} fusion(f32[8,2048,512]{2,1,0:T(8,128)} %get-tuple-element.160, f32[8,512]{1,0:T(8,128)S(1)} %select_maximum_fusion.2), kind=kLoop, calls=%fused_computation.4.clone.1 | loop fusion | flops 25161728 | bytes 33587200 | tf_op jit(solution)/shard_map/while/body/eval_jaxpr/reduce_sum | solution.py:52
  422.8 15.5 %fusion.53 = f32[8,512,128]{2,1,0:T(8,128)S(1)} fusion(f32[8,512,128]{2,1,0:T(8,128)S(1)} %get-tuple-element.178, bf16[8,4096,128]{2,1,0:T(8,128)(2,1)} %get-tuple-element.194, s32[]{:T(128)S(6)} %select_n.6, f32[8,2048,512]{2,1,0:T(8,128)} %get-tuple-element.160, f32[8,512]{1,0:T(8,128)S(1)} %select_maximum_fusion.2, ...), kind=kOutput, calls=%fused_computation.12.clone.1 | convolution fusion | flops 2174222336 | bytes 41975812 | tf_op jit(solution)/shard_map/while/body/eval_jaxpr/hqk,hkd->hqd/dot_general | solution.py:53
  438.4 0.6 dynamic_slice.26
  439.6 15.5 %bitcast_reduce_fusion.2 = (f32[8,512]{1,0:T(8,128)S(1)}, f32[8,2048,512]{2,1,0:T(8,128)}) fusion(bf16[8,512,128]{2,1,0:T(8,128)(2,1)S(1)} %get-tuple-element.193, bf16[8,4096,128]{2,1,0:T(8,128)(2,1)} %get-tuple-element.192, s32[]{:T(128)S(6)} %select_n.6), kind=kOutput, calls=%fused_computation.1.clone.1 | convolution fusion | flops 2164256768 | bytes 38813700 | tf_op jit(solution)/shard_map/while/body/eval_jaxpr/hqd,hkd->hqk/dot_general | solution.py:44
  455.1 13.6 %fusion.51 = f32[8,512]{1,0:T(8,128)S(1)} fusion(f32[8,2048,512]{2,1,0:T(8,128)} %get-tuple-element.160, f32[8,512]{1,0:T(8,128)S(1)} %select_maximum_fusion.2), kind=kLoop, calls=%fused_computation.4.clone.1 | loop fusion | flops 25161728 | bytes 33587200 | tf_op jit(solution)/shard_map/while/body/eval_jaxpr/reduce_sum | solution.py:52
  468.7 15.5 %fusion.53 = f32[8,512,128]{2,1,0:T(8,128)S(1)} fusion(f32[8,512,128]{2,1,0:T(8,128)S(1)} %get-tuple-element.178, bf16[8,4096,128]{2,1,0:T(8,128)(2,1)} %get-tuple-element.194, s32[]{:T(128)S(6)} %select_n.6, f32[8,2048,512]{2,1,0:T(8,128)} %get-tuple-element.160, f32[8,512]{1,0:T(8,128)S(1)} %select_maximum_fusion.2, ...), kind=kOutput, calls=%fused_computation.12.clone.1 | convolution fusion | flops 2174222336 | bytes 41975812 | tf_op jit(solution)/shard_map/while/body/eval_jaxpr/hqk,hkd->hqd/dot_general | solution.py:53
  484.3 0.0 copy-start.1
  484.3 1.3 copy-done.1
  485.6 1.9 copy.13
  487.6 1.2 divide_convert_fusion
  488.8 0.0 all-gather.13.cloned.1.call-update
  488.8 0.0 copy-start
  488.9 0.3 reduce-scatter.6.cloned.1.call-start
  489.1 8.6 %all-gather.13.cloned.1.call-done = bf16[512,2048]{0,1:T(8,128)(2,1)} async-done(((bf16[512,1024]{0,1:T(8,128)(2,1)}), bf16[512,2048]{0,1:T(8,128)(2,1)}) %all-gather.13.cloned.1.call-update) | async-done | bytes 2097168 | tf_op jit(solution)/shard_map/all_gather | solution.py:113
  497.8 13.0 %convolution_convert_fusion = bf16[512,3072]{1,0:T(8,128)(2,1)} fusion(bf16[512,2048]{0,1:T(8,128)(2,1)} %all-gather.13.cloned.1.call-done, bf16[2048,3072]{1,0:T(8,128)(2,1)} %param.11), kind=kOutput, calls=%fused_computation.33 | convolution fusion | flops 6444023808 | bytes 17825792 | tf_op jit(solution)/shard_map/dot_general | solution.py:112
  510.8 0.0 reduce-scatter.6.cloned.1.call-update
  510.8 44.8 %reduce-scatter.6.cloned.1.call-done = bf16[512,1536]{1,0:T(8,128)(2,1)} async-done(((bf16[512,3072]{1,0:T(8,128)(2,1)}), bf16[512,1536]{1,0:T(8,128)(2,1)}) %reduce-scatter.6.cloned.1.call-update) | async-done | bytes 1572880 | tf_op jit(solution)/shard_map/reduce_scatter | solution.py:117
  555.6 0.0 copy-done
  555.6 2.9 add_convert_fusion
  (13 shorter events, 0.1 us)
Async XLA Ops:
  6.5 50.0 %all-gather.11.cloned.1.call-start = ((), (), s32[]{:S(2)}) async-start(), calls=%async_computation.2 | async-start | bytes 4718592 | tf_op jit(solution)/shard_map/all_gather | solution.py:78
  7.3 128.0 %reduce-scatter.8.cloned.1.call-start = ((), (), s32[]{:S(2)}) async-start(), calls=%async_computation.7 | async-start | bytes 18874368
  114.4 153.4 %all-gather.17.cloned.1.call-start = ((), (), s32[]{:S(2)}) async-start(), calls=%async_computation.6 | async-start | bytes 9437184 | tf_op jit(solution)/shard_map/all_gather | solution.py:109
  140.8 251.7 %all-gather.15.cloned.1.call-start = ((), (), s32[]{:S(2)}) async-start(), calls=%async_computation.5 | async-start | bytes 9437184 | tf_op jit(solution)/shard_map/all_gather | solution.py:108
  141.4 356.4 %all-gather.13.cloned.1.call-start = ((), (), s32[]{:S(2)}) async-start(), calls=%async_computation.3 | async-start | bytes 3145728 | tf_op jit(solution)/shard_map/all_gather | solution.py:113
  484.3 1.4 copy-start.1
  488.8 66.8 %copy-start = (bf16[512,1536]{1,0:T(8,128)(2,1)S(1)}, bf16[512,1536]{1,0:T(8,128)(2,1)}, u32[]{:S(2)}) copy-start(bf16[512,1536]{1,0:T(8,128)(2,1)} %param.7) | copy-start | bytes 4718596
  488.9 66.7 %reduce-scatter.6.cloned.1.call-start = ((), (), s32[]{:S(2)}) async-start(), calls=%async_computation.4 | async-start | bytes 4718592 | tf_op jit(solution)/shard_map/reduce_scatter | solution.py:117
Sparse Core Ops, SparseCore 0:
  8.9 47.6 all-gather.10
  114.5 20.7 reduce-scatter.7
  140.9 126.8 all-gather.16
  269.8 122.6 all-gather.14
  489.0 8.7 all-gather.12
  511.0 44.5 reduce-scatter.5
where the time goes:
time: 566 us; the launch traced here: 565 us
  waiting for transfers between devices  365 us (64%)
  matrix products  103 us (18%)
  local copies, waits for them, and re-layouts  36.2 us (6%)
  other arithmetic  34.3 us (6%)
  between operations  13.5 us (2%)
  blocking collectives  12.2 us (2%)
    all_gather x1, waiting for transfers between devices, body(): lax.all_gather(owned[:, 2], 'seq', axis=1, tiled=True)  126 us
    all_gather x1, waiting for transfers between devices, body(): lax.all_gather(owned[:, 1], 'seq', axis=1, tiled=True)  125 us
    reduce_scatter x1, waiting for transfers between devices, body(): lax.psum_scatter(partial_output.astype(jnp.bfloat16), 'col', scatter_dime...  44.8 us
    all_gather x1, waiting for transfers between devices, body(): lax.all_gather(tokens, 'col', axis=1, tiled=True)  38.1 us
    unnamed x9, local copies, waits for them, and re-layouts  31.6 us
    dot_general x2, matrix products, fold_block(): jnp.einsum('hqk,' + key_form + '->hqd', weights.astype(jnp.bfloat16), val...  31.1 us
    dot_general x2, matrix products, fold_block(): jnp.einsum('hqd,' + key_form + '->hqk', queries, key_block, preferred_ele...  30.9 us
    dot_general x1, matrix products, body(): jnp.einsum('td,kdhe->hkte', normed, columns, preferred_element_type=jnp.f...  27.6 us
  transfers between devices with their start and end apart: 6, of which 6 were waited for; matrix products, arithmetic and copies ran while one was open for 0% of the time, Pallas kernels for 0%

commit v1 on v0

v1 whole, which is shorter than its diff:
```python
import functools
import math

import jax
import jax.numpy as jnp
from jax import lax
from jax.experimental import pallas as pl
from jax.experimental.pallas import tpu as pltpu
from jax.sharding import PartitionSpec as P

HD = 128
EPS = 0.25
IN_CHUNKS = 2
VMEM_LIMIT = 60 * 1024 * 1024


def params():
    return pltpu.CompilerParams(vmem_limit_bytes=VMEM_LIMIT)


def project_kernel(head_major, has_acc, idx_ref, x_ref, w_ref, *rest):
    if has_acc:
        acc_ref, out_ref = rest
    else:
        (out_ref,) = rest
    total = jnp.dot(x_ref[...], w_ref[0], preferred_element_type=jnp.float32)
    if has_acc:
        total = total + acc_ref[0]
    if head_major:
        for h in range(out_ref.shape[0]):
            out_ref[h, 0] = total[:, h * HD : (h + 1) * HD].astype(out_ref.dtype)
    else:
        out_ref[0] = total.astype(out_ref.dtype)


def project(x, w, acc, acc_row, row_block, col_block, width, dtype, head_major):
    rows, depth = x.shape
    bn = min(512, width)
    nb = width // bn
    idx = jnp.stack([jnp.int32(row_block), jnp.int32(col_block)])
    in_specs = [
        pl.BlockSpec((rows, depth), lambda k, j, i: (0, 0)),
        pl.BlockSpec((1, depth, bn), lambda k, j, i: (k, i[0], i[1] * nb + j)),
    ]
    args = [x, w]
    if acc is not None:
        in_specs.append(
            pl.BlockSpec((1, rows, bn), lambda k, j, i: (k, acc_row, i[1] * nb + j))
        )
        args.append(acc)
    if head_major:
        out_shape = jax.ShapeDtypeStruct((width // HD, 3, rows, HD), dtype)
        out_spec = pl.BlockSpec((bn // HD, 1, rows, HD), lambda k, j, i: (j, k, 0, 0))
    else:
        out_shape = jax.ShapeDtypeStruct((3, rows, width), dtype)
        out_spec = pl.BlockSpec((1, rows, bn), lambda k, j, i: (k, 0, j))
    return pl.pallas_call(
        functools.partial(project_kernel, head_major, acc is not None),
        grid_spec=pltpu.PrefetchScalarGridSpec(
            num_scalar_prefetch=1, grid=(3, nb), in_specs=in_specs, out_specs=out_spec
        ),
        out_shape=out_shape,
        compiler_params=params(),
        cost_estimate=pl.CostEstimate(
            flops=2 * rows * depth * width * 3,
            bytes_accessed=3 * width * (depth * 2 + rows * 8),
            transcendentals=0,
        ),
    )(idx, *args)


def attend_kernel(parts, q_ref, *refs):
    k_refs, v_refs, o_ref = refs[:parts], refs[parts : 2 * parts], refs[2 * parts]
    bs, tq = q_ref.shape[0], q_ref.shape[3]
    scale = math.log2(math.e) / math.sqrt(HD)
    q = q_ref[:, 0, 0].reshape(bs * tq, HD)
    top = acc = None
    for k_ref, v_ref in zip(k_refs, v_refs):
        sources, tk = k_ref.shape[0], k_ref.shape[3]
        step = max(1, min(sources, 1024 // tk))
        for first in range(0, sources, step):
            keys = k_ref[first : first + step, 0, 0].reshape(step * tk, HD)
            values = v_ref[first : first + step, 0, 0].reshape(step * tk, HD)
            values = jnp.concatenate([values, jnp.ones_like(values)], axis=1)
            scores = lax.dot_general(
                q, keys, (((1,), (1,)), ((), ())), preferred_element_type=jnp.float32
            )
            block_top = jnp.max(scores, axis=1, keepdims=True) * scale
            new_top = block_top if top is None else jnp.maximum(top, block_top)
            weights = jnp.exp2(scores * scale - new_top).astype(jnp.bfloat16)
            part = jnp.dot(weights, values, preferred_element_type=jnp.float32)
            acc = part if top is None else acc * jnp.exp2(top - new_top) + part
            top = new_top
    context = acc[:, :HD] / acc[:, HD:]
    o_ref[:, 0] = context.astype(o_ref.dtype).reshape(bs, tq, HD)


def attend(q, q_at, kvs, k_at):
    blocks, heads, _, tq, _ = q.shape
    bs = max(1, min(blocks, 512 // tq))

    def kv_spec(kv, at):
        shape = (kv.shape[0], 1, 1, kv.shape[3], HD)
        return pl.BlockSpec(shape, lambda h, i: (0, h, at, 0, 0))

    key_count = sum(kv.shape[0] * kv.shape[3] for kv in kvs)
    pairs = heads * blocks * tq * key_count
    return pl.pallas_call(
        functools.partial(attend_kernel, len(kvs)),
        grid=(heads, blocks // bs),
        in_specs=[pl.BlockSpec((bs, 1, 1, tq, HD), lambda h, i: (i, h, q_at, 0, 0))]
        + [kv_spec(kv, k_at) for kv in kvs]
        + [kv_spec(kv, k_at + 1) for kv in kvs],
        out_specs=pl.BlockSpec((bs, 1, tq, HD), lambda h, i: (i, h, 0, 0)),
        out_shape=jax.ShapeDtypeStruct((blocks, heads, tq, HD), jnp.bfloat16),
        compiler_params=params(),
        cost_estimate=pl.CostEstimate(
            flops=8 * pairs * HD,
            bytes_accessed=4 * heads * key_count * HD + 4 * heads * blocks * tq * HD,
            transcendentals=pairs,
        ),
    )(q, *kvs, *kvs)


def output_kernel(idx_ref, mine_ref, other_ref, w_ref, out_ref):
    def rows_of(ref):
        return jnp.concatenate([ref[h] for h in range(ref.shape[0])], axis=1)

    depth = mine_ref.shape[0] * HD
    mine_first = pl.multiple_of(idx_ref[0] * depth, depth)
    other_first = pl.multiple_of((1 - idx_ref[0]) * depth, depth)
    out_ref[...] = (
        jnp.dot(
            rows_of(mine_ref),
            w_ref[pl.ds(mine_first, depth), :],
            preferred_element_type=jnp.float32,
        )
        + jnp.dot(
            rows_of(other_ref),
            w_ref[pl.ds(other_first, depth), :],
            preferred_element_type=jnp.float32,
        )
    ).astype(out_ref.dtype)


def output_part(mine, other, w, row, col_block, width, dtype):
    heads, rows, _ = mine.shape
    bn = 512 if width % 512 == 0 else 256
    nb = width // bn
    idx = jnp.stack([jnp.int32(row), jnp.int32(col_block)])
    whole = pl.BlockSpec((heads, rows, HD), lambda j, i: (0, 0, 0))
    return pl.pallas_call(
        output_kernel,
        grid_spec=pltpu.PrefetchScalarGridSpec(
            num_scalar_prefetch=1,
            grid=(nb,),
            in_specs=[
                whole,
                whole,
                pl.BlockSpec((w.shape[0], bn), lambda j, i: (0, i[1] * nb + j)),
            ],
            out_specs=pl.BlockSpec((rows, bn), lambda j, i: (0, j)),
        ),
        out_shape=jax.ShapeDtypeStruct((rows, width), dtype),
        compiler_params=params(),
        cost_estimate=pl.CostEstimate(
            flops=2 * rows * w.shape[0] * width,
            bytes_accessed=width * (w.shape[0] * 2 + rows * 4),
            transcendentals=0,
        ),
    )(idx, mine, other, w)


def swap(x, axis):
    return lax.ppermute(x, axis, [(0, 1), (1, 0)])


def body(tokens, ln_gain, ln_bias, w_qkv, w_out):
    rows, quarter = tokens.shape
    row, col = lax.axis_index("row"), lax.axis_index("col")
    cols, seqs = lax.axis_size("col"), lax.axis_size("seq")
    model = quarter * cols * lax.axis_size("row")
    as_float = tokens.astype(jnp.float32)
    sums = lax.psum(
        jnp.stack([jnp.sum(as_float, axis=1), jnp.sum(as_float * as_float, axis=1)]),
        ("row", "col"),
    )
    token_mean = sums[0] / model
    spread = sums[1] / model - token_mean * token_mean
    normed = (
        (as_float - token_mean[:, None])
        * lax.rsqrt(spread + EPS)[:, None]
        * ln_gain.astype(jnp.float32)[None, :]
        + ln_bias.astype(jnp.float32)[None, :]
    ).astype(jnp.bfloat16)

    half = w_qkv.shape[2] // 2
    group_heads = half // HD
    by_head = group_heads % seqs == 0
    t_in = rows // IN_CHUNKS
    chunks = [normed[c * t_in : (c + 1) * t_in] for c in range(IN_CHUNKS)]
    if cols == 2:
        arrived = [swap(chunk, "col") for chunk in chunks]
        base = project(normed, w_qkv, None, 0, col, 0, 2 * half, jnp.float32, False)
        source = 1 - col
    else:
        arrived = [lax.all_gather(chunk, "col", axis=1, tiled=True) for chunk in chunks]
        base, source = None, 0

    owned = []
    for c in range(IN_CHUNKS):
        theirs = project(
            arrived[c], w_qkv, base, c, source, 1 - row, half, jnp.bfloat16, True
        )
        theirs = swap(theirs, "row")
        mine = project(arrived[c], w_qkv, base, c, source, row, half, jnp.float32, True)
        owned.append((mine + theirs.astype(jnp.float32)).astype(jnp.bfloat16))

    if by_head:
        split = [o.reshape(seqs, group_heads // seqs, 3, t_in, HD) for o in owned]
        split = [lax.all_to_all(o, "seq", 0, 0, tiled=True) for o in split]
        queries, kvs, k_at = split, split, 1
    else:
        queries = [o[None] for o in owned]
        kvs = [lax.all_gather(o[:, 1:], "seq", axis=0) for o in owned]
        k_at = 0

    finished = []
    for c in range(IN_CHUNKS):
        context = attend(queries[c], 0, kvs, k_at)
        if by_head:
            context = lax.all_to_all(context, "seq", 0, 0, tiled=True)
        context = context.reshape(group_heads, t_in, HD)
        other = swap(context, "row")
        residual = as_float[c * t_in : (c + 1) * t_in]
        if cols == 2:
            sent = output_part(context, other, w_out, row, 1 - col, quarter, jnp.bfloat16)
            sent = swap(sent, "col")
            kept = output_part(context, other, w_out, row, col, quarter, jnp.float32)
            summed = kept + sent.astype(jnp.float32)
        else:
            part = output_part(
                context, other, w_out, row, 0, w_out.shape[1], jnp.bfloat16
            )
            summed = lax.psum_scatter(
                part, "col", scatter_dimension=1, tiled=True
            ).astype(jnp.float32)
        finished.append((residual + summed).astype(jnp.bfloat16))
    return jnp.concatenate(finished, axis=0)


def solution(mesh):
    return jax.shard_map(
        body,
        mesh=mesh,
        in_specs=(
            P("seq", ("row", "col")),
            P(("row", "col")),
            P(("row", "col")),
            P(None, "row", "col"),
            P("col", "row"),
        ),
        out_specs=P("seq", ("row", "col")),
        check_vma=False,
    )
```

time: 566 us -> 248 us (0.44)
  waiting for transfers between devices: 365 us -> 39.8 us
  Pallas kernels: 0 us -> 114 us
  matrix products: 103 us -> 0 us
  blocking collectives: 12.2 us -> 49.6 us
  local copies, waits for them, and re-layouts: 36.2 us -> 4.28 us
  starting transfers between devices: 0.6 us -> 19.6 us
  other arithmetic: 34.3 us -> 19 us
  between operations: 13.5 us -> 0.13 us
    all_gather x4 -> x0, waiting for transfers between devices: 298 us -> none  [the longest x1 126 us: body(): lax.all_gather(owned[:, 2], 'seq', axis=1, tiled=True)]
    pallas_call x0 -> x11, Pallas kernels: none -> 114 us  [the longest x5 57.7 us: project(): pl.pallas_call(functools.partial(project_kernel, head_major, acc is not N...]
    dot_general x6 -> x0, matrix products: 103 us -> none  [the longest x2 31.1 us: fold_block(): jnp.einsum('hqk,' + key_form + '->hqd', weights.astype(jnp.bfloat16), val...]
    reduce_scatter x1 -> x0, waiting for transfers between devices: 44.8 us -> none  [body(): lax.psum_scatter(partial_output.astype(jnp.bfloat16), 'col', scatter_dime...]
    all_to_all x0 -> x1, blocking collectives: none -> 40.7 us  [body(): split = [lax.all_to_all(o, 'seq', 0, 0, tiled=True) for o in split]]
    unnamed x9 -> x22, local copies, waits for them, and re-layouts: 31.6 us -> 2.91 us
    all_to_all x0 -> x3, waiting for transfers between devices: none -> 28.5 us  [the longest x1 14.9 us: body(): split = [lax.all_to_all(o, 'seq', 0, 0, tiled=True) for o in split]]
    reduce_sum x2 -> x0, other arithmetic: 27.2 us -> none  [fold_block(): running_sum = running_sum * shrink + jnp.sum(weights, axis=2)]
  transfers between devices with their start and end apart: 6 -> 11, of which waited for: 6 -> 3; matrix products, arithmetic and copies ran while one was open for 0% -> 5% of each run, Pallas kernels for 0% -> 36%
where the time goes in v1:
time: 248 us; the launch traced here: 246 us
  Pallas kernels  114 us (46%)
  blocking collectives  49.6 us (20%)
  waiting for transfers between devices  39.8 us (16%)
  starting transfers between devices  19.6 us (8%)
  other arithmetic  19 us (8%)
  local copies, waits for them, and re-layouts  4.28 us (2%)
    pallas_call x5, Pallas kernels, project(): pl.pallas_call(functools.partial(project_kernel, head_major, acc is not N...  57.7 us
    all_to_all x1, blocking collectives, body(): split = [lax.all_to_all(o, 'seq', 0, 0, tiled=True) for o in split]  40.7 us
    pallas_call x2, Pallas kernels, attend(): pl.pallas_call(functools.partial(attend_kernel, len(kvs)), grid=(heads, b...  29.6 us
    pallas_call x4, Pallas kernels, output_part(): pl.pallas_call(output_kernel, grid_spec=pltpu.PrefetchScalarGridSpec(num_...  26.5 us
    all_to_all x1, waiting for transfers between devices, body(): split = [lax.all_to_all(o, 'seq', 0, 0, tiled=True) for o in split]  14.9 us
    all_to_all x2, waiting for transfers between devices, body(): context = lax.all_to_all(context, 'seq', 0, 0, tiled=True)  13.6 us
    ppermute x8, waiting for transfers between devices, swap(): return lax.ppermute(x, axis, [(0, 1), (1, 0)])  11.3 us
    all_to_all x2, starting transfers between devices, body(): context = lax.all_to_all(context, 'seq', 0, 0, tiled=True)  9.62 us
  transfers between devices with their start and end apart: 11, of which 3 were waited for; matrix products, arithmetic and copies ran while one was open for 5% of the time, Pallas kernels for 36%

profile of v1, /device:TPU:0, one launch (start us, length us, event | category | flops | bytes accessed | tf_op | source)
XLA Modules:
  0.0 246.2 jit_solution(17975180122212243743)
XLA Ops:
  0.0 0.0 copy-start
  0.0 0.0 copy-start.9
  0.0 0.0 copy-start.10
  0.0 2.1 convert_reduce_fusion
  2.1 9.0 %psum.7 = f32[2,512]{1,0:T(2,128)S(1)} all-reduce(f32[2,512]{1,0:T(2,128)S(1)} %pad_maximum_fusion.1), channel_id=1, replica_groups=mesh['seq'=8,'row'=2,'col'=2] {'row','col'}, use_global_device_ids=true, to_apply=%region_2.0 | all-reduce | flops 1024 | bytes 8192 | tf_op jit(solution)/shard_map/psum | solution.py:184
  11.1 0.0 copy-done.9
  11.1 0.0 copy-done.10
  11.1 0.0 copy-done
  11.1 0.6 add_convert_fusion.2.x_ref
  11.8 0.0 copy-start.1
  11.8 1.4 fusion.4
  13.2 0.3 copy-done.1
  13.5 0.6 collective-permute-start.2
  14.1 0.6 pad_add_fusion.2.idx_ref
  14.7 0.7 pad_add_fusion.3.idx_ref
  15.4 20.1 %shard_map.55.rest_0_ = f32[3,512,2048]{2,1,0:T(8,128)} custom-call(s32[2]{0:T(128)} %pad_add_fusion.2.idx_ref, bf16[512,1536]{1,0:T(8,128)(2,1)} %copy-done.1, bf16[3,3072,2048]{2,1,0:T(8,128)(2,1)} %w_ref.13), custom_call_target="tpu_custom_call" | custom-call | flops 9663676416 | bytes 44040192 | tf_op jit(solution)/shard_map/pallas_call | solution.py:57
  35.5 0.0 collective-permute-done.2.x_ref
  35.5 0.9 copy-done.5
  36.4 9.2 %shard_map.59 = bf16[8,3,256,128]{3,2,1,0:T(8,128)(2,1)} custom-call(s32[2]{0:T(128)} %pad_add_fusion.3.idx_ref, bf16[256,1536]{1,0:T(8,128)(2,1)} %copy-done.5, bf16[3,3072,2048]{2,1,0:T(8,128)(2,1)} %w_ref.13, f32[3,512,2048]{2,1,0:T(8,128)} %shard_map.55.rest_0_), custom_call_target="tpu_custom_call" | custom-call | flops 2415919104 | bytes 15728640 | tf_op jit(solution)/shard_map/pallas_call | solution.py:57
  45.6 0.0 collective-permute-start.3
  45.6 0.0 copy-done.8
  45.6 1.5 collective-permute-start
  47.1 0.7 pad_add_fusion.1.idx_ref
  47.8 9.6 %shard_map.58 = f32[8,3,256,128]{3,2,1,0:T(8,128)} custom-call(s32[2]{0:T(128)} %pad_add_fusion.1.idx_ref, bf16[256,1536]{1,0:T(8,128)(2,1)} %copy-done.5, bf16[3,3072,2048]{2,1,0:T(8,128)(2,1)} %w_ref.13, f32[3,512,2048]{2,1,0:T(8,128)} %shard_map.55.rest_0_), custom_call_target="tpu_custom_call" | custom-call | flops 2415919104 | bytes 15728640 | tf_op jit(solution)/shard_map/pallas_call | solution.py:57
  57.4 0.0 collective-permute-done.3
  57.4 4.0 %fusion.1 = bf16[8,1,3,256,128]{4,3,2,1,0:T(8,128)(2,1)} fusion(f32[8,3,256,128]{3,2,1,0:T(8,128)} %shard_map.58, bf16[8,3,256,128]{3,2,1,0:T(8,128)(2,1)} %collective-permute-done.3), kind=kLoop, calls=%fused_computation.6 | loop fusion | flops 2359296 | bytes 6291456 | tf_op jit(solution)/shard_map/reshape | solution.py:220
  61.4 5.8 %all-to-all-start.1 = ((bf16[8,1,3,256,128]{4,3,2,1,0:T(8,128)(2,1)}), bf16[8,1,3,256,128]{4,3,2,1,0:T(8,128)(2,1)}, u32[]{:S(2)}, u32[]{:S(2)}) async-start(bf16[8,1,3,256,128]{4,3,2,1,0:T(8,128)(2,1)} %fusion.1), calls=%async_computation.1 | async-start | bytes 3145728 | tf_op jit(solution)/shard_map/all_to_all | solution.py:221
  67.2 0.0 collective-permute-done.x_ref
  67.2 0.0 copy-start.6
  67.2 0.9 copy-done.6
  68.1 9.2 %shard_map.57 = bf16[8,3,256,128]{3,2,1,0:T(8,128)(2,1)} custom-call(s32[2]{0:T(128)} %pad_add_fusion.3.idx_ref, bf16[256,1536]{1,0:T(8,128)(2,1)} %copy-done.6, bf16[3,3072,2048]{2,1,0:T(8,128)(2,1)} %w_ref.13, f32[3,512,2048]{2,1,0:T(8,128)} %shard_map.55.rest_0_), custom_call_target="tpu_custom_call" | custom-call | flops 2415919104 | bytes 15728640 | tf_op jit(solution)/shard_map/pallas_call | solution.py:57
  77.3 0.0 collective-permute-start.1
  77.3 9.6 %shard_map.56 = f32[8,3,256,128]{3,2,1,0:T(8,128)} custom-call(s32[2]{0:T(128)} %pad_add_fusion.1.idx_ref, bf16[256,1536]{1,0:T(8,128)(2,1)} %copy-done.6, bf16[3,3072,2048]{2,1,0:T(8,128)(2,1)} %w_ref.13, f32[3,512,2048]{2,1,0:T(8,128)} %shard_map.55.rest_0_), custom_call_target="tpu_custom_call" | custom-call | flops 2415919104 | bytes 15728640 | tf_op jit(solution)/shard_map/pallas_call | solution.py:57
  86.9 0.0 collective-permute-done.1
  86.9 2.8 %fusion = bf16[8,1,3,256,128]{4,3,2,1,0:T(8,128)(2,1)S(1)} fusion(f32[8,3,256,128]{3,2,1,0:T(8,128)} %shard_map.56, bf16[8,3,256,128]{3,2,1,0:T(8,128)(2,1)} %collective-permute-done.1), kind=kLoop, calls=%fused_computation.5 | loop fusion | flops 2359296 | bytes 6291456 | tf_op jit(solution)/shard_map/reshape | solution.py:220
  89.7 14.9 %all-to-all-done.1.refs_1_.refs_3_.q_ref = bf16[8,1,3,256,128]{4,3,2,1,0:T(8,128)(2,1)} async-done(((bf16[8,1,3,256,128]{4,3,2,1,0:T(8,128)(2,1)}), bf16[8,1,3,256,128]{4,3,2,1,0:T(8,128)(2,1)}, u32[]{:S(2)}, u32[]{:S(2)}) %all-to-all-start.1) | async-done | bytes 1572896 | tf_op jit(solution)/shard_map/all_to_all | solution.py:221
  104.6 40.7 %all_to_all.20.q_ref.refs_0_.refs_2_ = bf16[8,1,3,256,128]{4,3,2,1,0:T(8,128)(2,1)} all-to-all(bf16[8,1,3,256,128]{4,3,2,1,0:T(8,128)(2,1)S(1)} %fusion), channel_id=1, replica_groups=mesh['seq'=8,'row'=2,'col'=2] {'seq'}, dimensions={0} | all-to-all | bytes 3145728 | tf_op jit(solution)/shard_map/all_to_all | solution.py:221
  145.2 14.8 %shard_map.63 = bf16[8,1,256,128]{3,2,1,0:T(8,128)(2,1)} custom-call(bf16[8,1,3,256,128]{4,3,2,1,0:T(8,128)(2,1)} %all-to-all-done.1.refs_1_.refs_3_.q_ref, bf16[8,1,3,256,128]{4,3,2,1,0:T(8,128)(2,1)} %all_to_all.20.q_ref.refs_0_.refs_2_, bf16[8,1,3,256,128]{4,3,2,1,0:T(8,128)(2,1)} %all-to-all-done.1.refs_1_.refs_3_.q_ref, ...), custom_call_target="tpu_custom_call" | custom-call | flops 8589934592 | bytes 3145728 | tf_op jit(solution)/shard_map/pallas_call | solution.py:108
  160.0 3.6 %all-to-all-start.3 = ((bf16[8,1,256,128]{3,2,1,0:T(8,128)(2,1)}), bf16[8,1,256,128]{3,2,1,0:T(8,128)(2,1)S(1)}, u32[]{:S(2)}, u32[]{:S(2)}) async-start(bf16[8,1,256,128]{3,2,1,0:T(8,128)(2,1)} %shard_map.63), calls=%async_computation.3 | async-start | bytes 1048576 | tf_op jit(solution)/shard_map/all_to_all | solution.py:232
  163.6 14.8 %shard_map.60 = bf16[8,1,256,128]{3,2,1,0:T(8,128)(2,1)} custom-call(bf16[8,1,3,256,128]{4,3,2,1,0:T(8,128)(2,1)} %all_to_all.20.q_ref.refs_0_.refs_2_, bf16[8,1,3,256,128]{4,3,2,1,0:T(8,128)(2,1)} %all_to_all.20.q_ref.refs_0_.refs_2_, bf16[8,1,3,256,128]{4,3,2,1,0:T(8,128)(2,1)} %all-to-all-done.1.refs_1_.refs_3_.q_ref, ...), custom_call_target="tpu_custom_call" | custom-call | flops 8589934592 | bytes 3145728 | tf_op jit(solution)/shard_map/pallas_call | solution.py:108
  178.5 0.0 all-to-all-done.3
  178.5 6.0 %all-to-all-start.2 = ((bf16[8,1,256,128]{3,2,1,0:T(8,128)(2,1)}), bf16[8,1,256,128]{3,2,1,0:T(8,128)(2,1)S(1)}, u32[]{:S(2)}, u32[]{:S(2)}) async-start(bf16[8,1,256,128]{3,2,1,0:T(8,128)(2,1)} %shard_map.60), calls=%async_computation.2 | async-start | bytes 1048576 | tf_op jit(solution)/shard_map/all_to_all | solution.py:232
  184.4 0.0 collective-permute-start.6
  184.5 13.6 %all-to-all-done.2 = bf16[8,1,256,128]{3,2,1,0:T(8,128)(2,1)S(1)} async-done(((bf16[8,1,256,128]{3,2,1,0:T(8,128)(2,1)}), bf16[8,1,256,128]{3,2,1,0:T(8,128)(2,1)S(1)}, u32[]{:S(2)}, u32[]{:S(2)}) %all-to-all-start.2) | async-done | bytes 524320 | tf_op jit(solution)/shard_map/all_to_all | solution.py:232
  198.0 0.0 collective-permute-start.4
  198.0 0.7 pad_add_fusion.4.idx_ref
  198.7 0.0 collective-permute-done.6.other_ref
  198.7 0.0 copy-done.3
  198.7 6.4 %shard_map.65 = bf16[256,1536]{1,0:T(8,128)(2,1)} custom-call(s32[2]{0:T(128)} %pad_add_fusion.4.idx_ref, bf16[8,256,128]{2,1,0:T(8,128)(2,1)} %bitcast.15, bf16[8,256,128]{2,1,0:T(8,128)(2,1)} %collective-permute-done.6.other_ref, bf16[2048,3072]{1,0:T(8,128)(2,1)} %w_ref.17), custom_call_target="tpu_custom_call" | custom-call | flops 1610612736 | bytes 7864320 | tf_op jit(solution)/shard_map/pallas_call | solution.py:152
  205.1 0.0 copy-done.4
  205.1 1.1 collective-permute-start.7
  206.2 0.0 collective-permute-done.4.other_ref
  206.2 0.8 copy-done.7
  207.0 6.4 %shard_map.62 = bf16[256,1536]{1,0:T(8,128)(2,1)} custom-call(s32[2]{0:T(128)} %pad_add_fusion.4.idx_ref, bf16[8,256,128]{2,1,0:T(8,128)(2,1)} %bitcast.18, bf16[8,256,128]{2,1,0:T(8,128)(2,1)} %copy-done.7, bf16[2048,3072]{1,0:T(8,128)(2,1)} %w_ref.17), custom_call_target="tpu_custom_call" | custom-call | flops 1610612736 | bytes 7864320 | tf_op jit(solution)/shard_map/pallas_call | solution.py:152
  213.4 0.9 collective-permute-start.5
  214.3 2.1 convert_element_type.36
  216.4 0.6 pad_add_fusion.idx_ref
  217.0 6.8 %shard_map.64 = f32[256,1536]{1,0:T(8,128)} custom-call(s32[2]{0:T(128)} %pad_add_fusion.idx_ref, bf16[8,256,128]{2,1,0:T(8,128)(2,1)} %bitcast.16, bf16[8,256,128]{2,1,0:T(8,128)(2,1)} %collective-permute-done.6.other_ref, bf16[2048,3072]{1,0:T(8,128)(2,1)} %w_ref.17), custom_call_target="tpu_custom_call" | custom-call | flops 1610612736 | bytes 7864320 | tf_op jit(solution)/shard_map/pallas_call | solution.py:152
  223.8 7.0 %shard_map.61 = f32[256,1536]{1,0:T(8,128)} custom-call(s32[2]{0:T(128)} %pad_add_fusion.idx_ref, bf16[8,256,128]{2,1,0:T(8,128)(2,1)} %bitcast.19, bf16[8,256,128]{2,1,0:T(8,128)(2,1)} %copy-done.7, bf16[2048,3072]{1,0:T(8,128)(2,1)} %w_ref.17), custom_call_target="tpu_custom_call" | custom-call | flops 1610612736 | bytes 7864320 | tf_op jit(solution)/shard_map/pallas_call | solution.py:152
  230.7 0.0 collective-permute-done.7
  230.7 11.3 %collective-permute-done.5 = bf16[256,1536]{1,0:T(8,128)(2,1)S(1)} collective-permute-done((bf16[256,1536]{1,0:T(8,128)(2,1)}, bf16[256,1536]{1,0:T(8,128)(2,1)S(1)}, u32[]{:S(2)}, u32[]{:S(2)}) %collective-permute-start.5) | collective-permute-done | bytes 786464 | tf_op jit(solution)/shard_map/ppermute | solution.py:175
  242.0 0.0 copy-done.2
  242.1 2.9 %fusion.3 = (bf16[256,1536]{1,0:T(8,128)(2,1)S(1)}, bf16[256,1536]{1,0:T(8,128)(2,1)S(1)}) fusion(f32[512,1536]{1,0:T(8,128)S(1)} %copy-done.2, f32[256,1536]{1,0:T(8,128)} %shard_map.61, bf16[256,1536]{1,0:T(8,128)(2,1)S(1)} %collective-permute-done.5, f32[256,1536]{1,0:T(8,128)} %shard_map.64, bf16[256,1536]{1,0:T(8,128)(2,1)} %collective-permute-done.7), kind=kLoop, calls=%fused_computation.10 | loop fusion | flops 3145728 | bytes 9437184 | tf_op jit(solution)/shard_map/convert_element_type | solution.py:248
  245.0 1.2 pad_maximum_fusion
  (11 shorter events, 0.0 us)
Async XLA Ops:
  0.0 11.1 %copy-start = (bf16[512,1536]{1,0:T(8,128)(2,1)S(1)}, bf16[512,1536]{1,0:T(8,128)(2,1)}, u32[]{:S(2)}) copy-start(bf16[512,1536]{1,0:T(8,128)(2,1)} %param.5) | copy-start | bytes 4718596
  0.0 11.1 %copy-start.9 = (bf16[1536]{0:T(1024)(128)(2,1)S(1)}, bf16[1536]{0:T(1024)(128)(2,1)}, u32[]{:S(2)}) copy-start(bf16[1536]{0:T(1024)(128)(2,1)} %param.6) | copy-start | bytes 9220
  0.0 11.1 %copy-start.10 = (bf16[1536]{0:T(1024)(128)(2,1)S(1)}, bf16[1536]{0:T(1024)(128)(2,1)}, u32[]{:S(2)}) copy-start(bf16[1536]{0:T(1024)(128)(2,1)} %param.7) | copy-start | bytes 9220
  11.8 1.7 copy-start.1
  13.5 22.0 %collective-permute-start.2 = (bf16[256,1536]{1,0:T(8,128)(2,1)}, bf16[256,1536]{1,0:T(8,128)(2,1)S(1)}, u32[]{:S(2)}, u32[]{:S(2)}) collective-permute-start(bf16[256,1536]{1,0:T(8,128)(2,1)} %get-tuple-element.10), channel_id=1, source_target_pairs={{0,1},{1,0},{2,3},{3,2},{4,5},{5,4},{6,7},{7,6},{8,9},{9,8},{10,11... | collective-permute-start | bytes 2359304 | tf_op jit(solution)/shard_map/ppermute | solution.py:175
  35.5 10.1 %copy-start.8 = (bf16[256,1536]{1,0:T(8,128)(2,1)S(1)}, bf16[256,1536]{1,0:T(8,128)(2,1)}, u32[]{:S(2)}) copy-start(bf16[256,1536]{1,0:T(8,128)(2,1)} %get-tuple-element.9) | copy-start | bytes 2359300
  35.5 0.9 copy-start.5
  45.6 11.8 %collective-permute-start.3 = (bf16[8,3,256,128]{3,2,1,0:T(8,128)(2,1)}, bf16[8,3,256,128]{3,2,1,0:T(8,128)(2,1)}, u32[]{:S(2)}, u32[]{:S(2)}) collective-permute-start(bf16[8,3,256,128]{3,2,1,0:T(8,128)(2,1)} %shard_map.59), channel_id=1, source_target_pairs={{0,2},{2,0},{1,3},{3,1},{4,6},{6,4},{5,7},{7,5},{8,10},{10,8},{9,1... | collective-permute-start | bytes 4718600 | tf_op jit(solution)/shard_map/ppermute | solution.py:175
  45.6 21.6 %collective-permute-start = (bf16[256,1536]{1,0:T(8,128)(2,1)S(1)}, bf16[256,1536]{1,0:T(8,128)(2,1)S(1)}, u32[]{:S(2)}, u32[]{:S(2)}) collective-permute-start(bf16[256,1536]{1,0:T(8,128)(2,1)S(1)} %copy-done.8), channel_id=1, source_target_pairs={{0,1},{1,0},{2,3},{3,2},{4,5},{5,4},{6,7},{7,6},{8,9},{9,8},{10,11... | collective-permute-start | bytes 2359304 | tf_op jit(solution)/shard_map/ppermute | solution.py:175
  61.4 43.2 %all-to-all-start.1 = ((bf16[8,1,3,256,128]{4,3,2,1,0:T(8,128)(2,1)}), bf16[8,1,3,256,128]{4,3,2,1,0:T(8,128)(2,1)}, u32[]{:S(2)}, u32[]{:S(2)}) async-start(bf16[8,1,3,256,128]{4,3,2,1,0:T(8,128)(2,1)} %fusion.1), calls=%async_computation.1 | async-start | bytes 3145728 | tf_op jit(solution)/shard_map/all_to_all | solution.py:221
  67.2 0.9 copy-start.6
  77.3 9.6 %collective-permute-start.1 = (bf16[8,3,256,128]{3,2,1,0:T(8,128)(2,1)}, bf16[8,3,256,128]{3,2,1,0:T(8,128)(2,1)}, u32[]{:S(2)}, u32[]{:S(2)}) collective-permute-start(bf16[8,3,256,128]{3,2,1,0:T(8,128)(2,1)} %shard_map.57), channel_id=1, source_target_pairs={{0,2},{2,0},{1,3},{3,1},{4,6},{6,4},{5,7},{7,5},{8,10},{10,8},{9,1... | collective-permute-start | bytes 4718600 | tf_op jit(solution)/shard_map/ppermute | solution.py:175
  160.0 18.5 %all-to-all-start.3 = ((bf16[8,1,256,128]{3,2,1,0:T(8,128)(2,1)}), bf16[8,1,256,128]{3,2,1,0:T(8,128)(2,1)S(1)}, u32[]{:S(2)}, u32[]{:S(2)}) async-start(bf16[8,1,256,128]{3,2,1,0:T(8,128)(2,1)} %shard_map.63), calls=%async_computation.3 | async-start | bytes 1048576 | tf_op jit(solution)/shard_map/all_to_all | solution.py:232
  178.5 20.3 %copy-start.3 = (bf16[8,1,256,128]{3,2,1,0:T(8,128)(2,1)}, bf16[8,1,256,128]{3,2,1,0:T(8,128)(2,1)S(1)}, u32[]{:S(2)}) copy-start(bf16[8,1,256,128]{3,2,1,0:T(8,128)(2,1)S(1)} %all-to-all-done.3) | copy-start | bytes 1572868
  178.5 19.6 %all-to-all-start.2 = ((bf16[8,1,256,128]{3,2,1,0:T(8,128)(2,1)}), bf16[8,1,256,128]{3,2,1,0:T(8,128)(2,1)S(1)}, u32[]{:S(2)}, u32[]{:S(2)}) async-start(bf16[8,1,256,128]{3,2,1,0:T(8,128)(2,1)} %shard_map.60), calls=%async_computation.2 | async-start | bytes 1048576 | tf_op jit(solution)/shard_map/all_to_all | solution.py:232
  184.4 14.3 %collective-permute-start.6 = (bf16[8,256,128]{2,1,0:T(8,128)(2,1)S(1)}, bf16[8,256,128]{2,1,0:T(8,128)(2,1)}, u32[]{:S(2)}, u32[]{:S(2)}) collective-permute-start(bf16[8,256,128]{2,1,0:T(8,128)(2,1)S(1)} %bitcast.14), channel_id=1, source_target_pairs={{0,2},{2,0},{1,3},{3,1},{4,6},{6,4},{5,7},{7,5},{8,10},{10,8},{9,1... | collective-permute-start | bytes 1572872 | tf_op jit(solution)/shard_map/ppermute | solution.py:175
  198.0 7.1 %copy-start.4 = (bf16[8,1,256,128]{3,2,1,0:T(8,128)(2,1)}, bf16[8,1,256,128]{3,2,1,0:T(8,128)(2,1)S(1)}, u32[]{:S(2)}) copy-start(bf16[8,1,256,128]{3,2,1,0:T(8,128)(2,1)S(1)} %all-to-all-done.2) | copy-start | bytes 1572868
  198.0 8.2 %collective-permute-start.4 = (bf16[8,256,128]{2,1,0:T(8,128)(2,1)S(1)}, bf16[8,256,128]{2,1,0:T(8,128)(2,1)S(1)}, u32[]{:S(2)}, u32[]{:S(2)}) collective-permute-start(bf16[8,256,128]{2,1,0:T(8,128)(2,1)S(1)} %bitcast.17), channel_id=1, source_target_pairs={{0,2},{2,0},{1,3},{3,1},{4,6},{6,4},{5,7},{7,5},{8,10},{10,8},{9,1... | collective-permute-start | bytes 1572872 | tf_op jit(solution)/shard_map/ppermute | solution.py:175
  205.1 25.7 %collective-permute-start.7 = (bf16[256,1536]{1,0:T(8,128)(2,1)}, bf16[256,1536]{1,0:T(8,128)(2,1)}, u32[]{:S(2)}, u32[]{:S(2)}) collective-permute-start(bf16[256,1536]{1,0:T(8,128)(2,1)} %shard_map.65), channel_id=1, source_target_pairs={{0,1},{1,0},{2,3},{3,2},{4,5},{5,4},{6,7},{7,6},{8,9},{9,8},{10,11... | collective-permute-start | bytes 2359304 | tf_op jit(solution)/shard_map/ppermute | solution.py:175
  206.2 0.8 copy-start.7
  213.4 28.6 %collective-permute-start.5 = (bf16[256,1536]{1,0:T(8,128)(2,1)}, bf16[256,1536]{1,0:T(8,128)(2,1)S(1)}, u32[]{:S(2)}, u32[]{:S(2)}) collective-permute-start(bf16[256,1536]{1,0:T(8,128)(2,1)} %shard_map.62), channel_id=1, source_target_pairs={{0,1},{1,0},{2,3},{3,2},{4,5},{5,4},{6,7},{7,6},{8,9},{9,8},{10,11... | collective-permute-start | bytes 2359304 | tf_op jit(solution)/shard_map/ppermute | solution.py:175
  223.8 18.3 %copy-start.2 = (f32[512,1536]{1,0:T(8,128)S(1)}, f32[512,1536]{1,0:T(8,128)}, u32[]{:S(2)}) copy-start(f32[512,1536]{1,0:T(8,128)} %convert_element_type.36) | copy-start | bytes 9437188

commit v2 on v1

v2 whole, which is shorter than its diff:
```python
import functools
import math

import jax
import jax.numpy as jnp
from jax import lax
from jax.experimental import pallas as pl
from jax.experimental.pallas import tpu as pltpu
from jax.sharding import PartitionSpec as P


HD = 128
EPS = 0.25
SIXTEENTHS = (7, 5, 4)
CHUNKS = len(SIXTEENTHS)
OUT_GROUPS = ((0,), (1,), (2,))
VMEM_LIMIT = 60 * 1024 * 1024


def params():
    return pltpu.CompilerParams(vmem_limit_bytes=VMEM_LIMIT)


def project_kernel(parts, idx_ref, *refs):
    x_refs, (w_ref, theirs_ref, mine_ref) = refs[:parts], refs[parts:]
    total = None
    for p, x_ref in enumerate(x_refs):
        depth = x_ref.shape[1]
        first = pl.multiple_of(idx_ref[p] * depth, depth)
        term = jnp.dot(
            x_ref[...], w_ref[0, pl.ds(first, depth), :], preferred_element_type=jnp.float32
        )
        total = term if total is None else total + term
    total = total.astype(jnp.bfloat16)

    def store(ref):
        for h in range(ref.shape[0]):
            ref[h, 0] = total[:, h * HD : (h + 1) * HD]

    pl.when(pl.program_id(0) == 0)(lambda: store(theirs_ref))
    pl.when(pl.program_id(0) == 1)(lambda: store(mine_ref))


def project(xs, row_blocks, w, row):
    rows = xs[0].shape[0]
    depth, width = w.shape[1], w.shape[2] // 2
    bn = min(1024, width)
    nb = width // bn
    parts = len(xs)
    idx = jnp.stack([jnp.int32(i) for i in (*row_blocks, 1 - row, row)])
    block = (bn // HD, 1, rows, HD)
    shape = jax.ShapeDtypeStruct((width // HD, 3, rows, HD), jnp.bfloat16)

    def theirs_at(s, k, j, i):
        return (jnp.where(s == 0, j, nb - 1), jnp.where(s == 0, k, 2), 0, 0)

    def mine_at(s, k, j, i):
        return (jnp.where(s == 0, 0, j), jnp.where(s == 0, 0, k), 0, 0)

    return pl.pallas_call(
        functools.partial(project_kernel, parts),
        grid_spec=pltpu.PrefetchScalarGridSpec(
            num_scalar_prefetch=1,
            grid=(2, 3, nb),
            in_specs=[pl.BlockSpec(x.shape, lambda s, k, j, i: (0, 0)) for x in xs]
            + [
                pl.BlockSpec(
                    (1, depth, bn), lambda s, k, j, i: (k, 0, i[parts + s] * nb + j)
                )
            ],
            out_specs=[pl.BlockSpec(block, theirs_at), pl.BlockSpec(block, mine_at)],
        ),
        out_shape=[shape, shape],
        compiler_params=params(),
        name="project",
        cost_estimate=pl.CostEstimate(
            flops=12 * rows * depth * width,
            bytes_accessed=12 * depth * width,
            transcendentals=0,
        ),
    )(idx, *xs, w)


def divisor(count, most):
    return next(n for n in range(max(1, min(count, most)), 0, -1) if count % n == 0)


def attend_kernel(parts, carried, final, q_ref, *refs):
    k_refs, v_refs, refs = refs[:parts], refs[parts : 2 * parts], refs[2 * parts :]
    bs, tq = q_ref.shape[0], q_ref.shape[3]
    scale = math.log2(math.e) / math.sqrt(HD)
    q = q_ref[:, 0, 0].reshape(bs * tq, HD)
    top = acc = None
    if carried:
        acc = refs[0][:, 0].reshape(bs * tq, 2 * HD)
        top = refs[1][:, 0].reshape(bs * tq, HD)[:, :1]
        refs = refs[2:]
    for k_ref, v_ref in zip(k_refs, v_refs):
        sources, tk = k_ref.shape[0], k_ref.shape[3]
        step = divisor(sources, 1024 // tk)
        for first in range(0, sources, step):
            keys = k_ref[first : first + step, 0, 0].reshape(step * tk, HD)
            values = v_ref[first : first + step, 0, 0].reshape(step * tk, HD)
            values = jnp.concatenate([values, jnp.ones_like(values)], axis=1)
            scores = lax.dot_general(
                q, keys, (((1,), (1,)), ((), ())), preferred_element_type=jnp.float32
            )
            block_top = jnp.max(scores, axis=1, keepdims=True) * scale
            new_top = block_top if top is None else jnp.maximum(top, block_top)
            weights = jnp.exp2(scores * scale - new_top).astype(jnp.bfloat16)
            part = jnp.dot(weights, values, preferred_element_type=jnp.float32)
            acc = part if top is None else acc * jnp.exp2(top - new_top) + part
            top = new_top
    if final:
        context = acc[:, :HD] / acc[:, HD:]
        refs[0][:, 0] = context.astype(jnp.bfloat16).reshape(bs, tq, HD)
    else:
        refs[0][:, 0] = acc.reshape(bs, tq, 2 * HD)
        refs[1][:, 0] = jnp.broadcast_to(top, (bs * tq, HD)).reshape(bs, tq, HD)


def attend(q, q_at, kvs, k_at, state=None, final=True):
    blocks, heads, _, tq, _ = q.shape
    bs = divisor(blocks, 1024 // tq)

    def kv_spec(kv, at):
        shape = (kv.shape[0], 1, 1, kv.shape[3], HD)
        return pl.BlockSpec(shape, lambda h, i: (0, h, at, 0, 0))

    def row_spec(width):
        return pl.BlockSpec((bs, 1, tq, width), lambda h, i: (i, h, 0, 0))

    def row_shape(width, dtype):
        return jax.ShapeDtypeStruct((blocks, heads, tq, width), dtype)

    state_specs = [row_spec(2 * HD), row_spec(HD)]
    key_count = sum(kv.shape[0] * kv.shape[3] for kv in kvs)
    pairs = heads * blocks * tq * key_count
    return pl.pallas_call(
        functools.partial(attend_kernel, len(kvs), state is not None, final),
        grid=(heads, blocks // bs),
        in_specs=[pl.BlockSpec((bs, 1, 1, tq, HD), lambda h, i: (i, h, q_at, 0, 0))]
        + [kv_spec(kv, k_at) for kv in kvs]
        + [kv_spec(kv, k_at + 1) for kv in kvs]
        + ([] if state is None else state_specs),
        out_specs=row_spec(HD) if final else state_specs,
        out_shape=row_shape(HD, jnp.bfloat16)
        if final
        else [row_shape(2 * HD, jnp.float32), row_shape(HD, jnp.float32)],
        name="attend",
        compiler_params=params(),
        cost_estimate=pl.CostEstimate(
            flops=8 * pairs * HD,
            bytes_accessed=4 * heads * key_count * HD + 4 * heads * blocks * tq * HD,
            transcendentals=pairs,
        ),
    )(q, *kvs, *kvs, *(() if state is None else state))


def output_kernel(idx_ref, mine_ref, other_ref, w_ref, out_ref):
    def rows_of(ref):
        return jnp.concatenate([ref[h] for h in range(ref.shape[0])], axis=1)

    depth = mine_ref.shape[0] * HD
    mine_first = pl.multiple_of(idx_ref[0] * depth, depth)
    other_first = pl.multiple_of((1 - idx_ref[0]) * depth, depth)
    out_ref[...] = (
        jnp.dot(
            rows_of(mine_ref),
            w_ref[pl.ds(mine_first, depth), :],
            preferred_element_type=jnp.float32,
        )
        + jnp.dot(
            rows_of(other_ref),
            w_ref[pl.ds(other_first, depth), :],
            preferred_element_type=jnp.float32,
        )
    ).astype(out_ref.dtype)


def output_part(mine, other, w, row, col_block, width, dtype):
    heads, rows, _ = mine.shape
    bn = next(n for n in (768, 512, 256) if width % n == 0)
    nb = width // bn
    idx = jnp.stack([jnp.int32(row), jnp.int32(col_block)])
    whole = pl.BlockSpec((heads, rows, HD), lambda j, i: (0, 0, 0))
    return pl.pallas_call(
        output_kernel,
        grid_spec=pltpu.PrefetchScalarGridSpec(
            num_scalar_prefetch=1,
            grid=(nb,),
            in_specs=[
                whole,
                whole,
                pl.BlockSpec((w.shape[0], bn), lambda j, i: (0, i[1] * nb + j)),
            ],
            out_specs=pl.BlockSpec((rows, bn), lambda j, i: (0, j)),
        ),
        out_shape=jax.ShapeDtypeStruct((rows, width), dtype),
        name="output_part",
        compiler_params=params(),
        cost_estimate=pl.CostEstimate(
            flops=2 * rows * w.shape[0] * width,
            bytes_accessed=width * (w.shape[0] * 2 + rows * 4),
            transcendentals=0,
        ),
    )(idx, mine, other, w)


def swap(x, axis):
    return lax.ppermute(x, axis, [(0, 1), (1, 0)])


def body(tokens, ln_gain, ln_bias, w_qkv, w_out):
    rows, quarter = tokens.shape
    row, col = lax.axis_index("row"), lax.axis_index("col")
    cols, seqs = lax.axis_size("col"), lax.axis_size("seq")
    model = quarter * cols * lax.axis_size("row")
    half = w_qkv.shape[2] // 2
    group_heads = half // HD
    by_head = group_heads % seqs == 0
    bounds = [rows * sum(SIXTEENTHS[:c]) // 16 for c in range(CHUNKS + 1)]
    pieces = [tokens[bounds[c] : bounds[c + 1]] for c in range(CHUNKS)]
    features = quarter
    scales = jnp.concatenate([ln_gain, ln_bias])
    if cols == 2:
        arrived = []
        for piece in pieces:
            arrived.append([piece, swap(piece, "col")])
        scales = [scales, swap(scales, "col")]
        blocks = [col, 1 - col]
    else:
        arrived = [[lax.all_gather(piece, "col", axis=1, tiled=True)] for piece in pieces]
        gathered = lax.all_gather(scales.reshape(2, quarter), "col", axis=1, tiled=True)
        features = quarter * cols
        scales = [gathered.reshape(2 * features)]
        blocks = [0]

    owned = []
    for held in arrived:
        floats = [x.astype(jnp.float32) for x in held]
        sums = jnp.stack(
            [
                sum(jnp.sum(x, axis=1) for x in floats),
                sum(jnp.sum(x * x, axis=1) for x in floats),
            ]
        )
        sums = (sums + swap(sums, "row")) / model
        inverse = lax.rsqrt(sums[1] - sums[0] * sums[0] + EPS)
        normed = [
            (
                (x - sums[0][:, None])
                * inverse[:, None]
                * scale[:features].astype(jnp.float32)[None, :]
                + scale[features:].astype(jnp.float32)[None, :]
            ).astype(jnp.bfloat16)
            for x, scale in zip(floats, scales)
        ]
        theirs, mine = project(normed, blocks, w_qkv, row)
        theirs = swap(theirs, "row")
        owned.append(
            (mine.astype(jnp.float32) + theirs.astype(jnp.float32)).astype(jnp.bfloat16)
        )

    if by_head:
        split = [o.reshape(seqs, group_heads // seqs, *o.shape[1:]) for o in owned]
        for c, o in enumerate(split):
            split[c] = lax.all_to_all(o, "seq", 0, 0, tiled=True)
        queries, kvs, k_at = split, split, 1
    else:
        queries = [o[None] for o in owned]
        kvs = [lax.all_gather(o[:, 1:], "seq", axis=0) for o in owned]
        k_at = 0

    states = []
    for c in range(CHUNKS - 1):
        states.append(attend(queries[c], 0, kvs[:-1], k_at, None, False))

    finished = []
    for group in OUT_GROUPS:
        contexts = []
        for c in group:
            if c < CHUNKS - 1:
                contexts.append(attend(queries[c], 0, kvs[-1:], k_at, states[c]))
            else:
                contexts.append(attend(queries[c], 0, kvs, k_at))
        context = jnp.concatenate(contexts, axis=2)
        first, last = bounds[group[0]], bounds[group[-1] + 1]
        if by_head:
            context = lax.all_to_all(context, "seq", 0, 0, tiled=True)
        context = context.reshape(group_heads, last - first, HD)
        other = swap(context, "row")
        if cols == 2:
            sent = output_part(
                context, other, w_out, row, 1 - col, quarter, jnp.bfloat16
            )
            sent = swap(sent, "col")
            kept = output_part(context, other, w_out, row, col, quarter, jnp.float32)
            summed = kept + sent.astype(jnp.float32)
        else:
            part = output_part(
                context, other, w_out, row, 0, w_out.shape[1], jnp.bfloat16
            )
            summed = lax.psum_scatter(
                part, "col", scatter_dimension=1, tiled=True
            ).astype(jnp.float32)
        residual = tokens[first:last].astype(jnp.float32)
        finished.append((residual + summed).astype(jnp.bfloat16))
    return jnp.concatenate(finished, axis=0)


def solution(mesh):
    return jax.shard_map(
        body,
        mesh=mesh,
        in_specs=(
            P("seq", ("row", "col")),
            P(("row", "col")),
            P(("row", "col")),
            P(None, "row", "col"),
            P("col", "row"),
        ),
        out_specs=P("seq", ("row", "col")),
        check_vma=False,
    )
```

time: 248 us -> 281 us (1.13)
  starting transfers between devices: 19.6 us -> 34.8 us
  waiting for transfers between devices: 39.8 us -> 54.4 us
  blocking collectives: 49.6 us -> 38.5 us
  Pallas kernels: 114 us -> 125 us
    ppermute x8 -> x16, waiting for transfers between devices: 11.3 us -> 24.9 us  [swap(): return lax.ppermute(x, axis, [(0, 1), (1, 0)])]
    psum x1 -> x0, blocking collectives: 8.96 us -> none  [body(): lax.psum(jnp.stack([jnp.sum(as_float, axis=1), jnp.sum(as_float * as_floa...]
    pallas_call x7 -> x8, Pallas kernels: 87.3 us -> 93.4 us  [the longest x3 50.2 us: project(): pl.pallas_call(functools.partial(project_kernel, parts), grid_spec=pltpu....]
    all_to_all x2 -> x3, starting transfers between devices: 9.62 us -> 15.4 us  [body(): context = lax.all_to_all(context, 'seq', 0, 0, tiled=True)]
    ppermute x8 -> x16, starting transfers between devices: 4.17 us -> 9.46 us  [swap(): return lax.ppermute(x, axis, [(0, 1), (1, 0)])]
    pallas_call x4 -> x6, Pallas kernels: 26.5 us -> 31.5 us  [output_part(): pl.pallas_call(output_kernel, grid_spec=pltpu.PrefetchScalarGridSpec(num_...]
    all_to_all x1 -> x2, starting transfers between devices: 5.8 us -> 10 us  [body(): split[c] = lax.all_to_all(o, 'seq', 0, 0, tiled=True)]
    all_to_all x1 -> x2, waiting for transfers between devices: 14.9 us -> 18.5 us  [body(): split[c] = lax.all_to_all(o, 'seq', 0, 0, tiled=True)]
  transfers between devices with their start and end apart: 11 -> 21, of which waited for: 3 -> 8; matrix products, arithmetic and copies ran while one was open for 5% -> 8% of each run, Pallas kernels for 36% -> 42%
where the time goes in v2:
time: 281 us; the launch traced here: 280 us
  Pallas kernels  125 us (44%)
  waiting for transfers between devices  54.4 us (19%)
  blocking collectives  38.5 us (14%)
  starting transfers between devices  34.8 us (12%)
  other arithmetic  20.8 us (7%)
  local copies, waits for them, and re-layouts  6.01 us (2%)
    pallas_call x3, Pallas kernels, project(): pl.pallas_call(functools.partial(project_kernel, parts), grid_spec=pltpu....  50.2 us
    pallas_call x5, Pallas kernels, attend(): pl.pallas_call(functools.partial(attend_kernel, len(kvs), state is not No...  43.1 us
    all_to_all x1, blocking collectives, body(): split[c] = lax.all_to_all(o, 'seq', 0, 0, tiled=True)  38.5 us
    pallas_call x6, Pallas kernels, output_part(): pl.pallas_call(output_kernel, grid_spec=pltpu.PrefetchScalarGridSpec(num_...  31.5 us
    ppermute x16, waiting for transfers between devices, swap(): return lax.ppermute(x, axis, [(0, 1), (1, 0)])  24.9 us
    all_to_all x2, waiting for transfers between devices, body(): split[c] = lax.all_to_all(o, 'seq', 0, 0, tiled=True)  18.5 us
    all_to_all x3, starting transfers between devices, body(): context = lax.all_to_all(context, 'seq', 0, 0, tiled=True)  15.4 us
    all_to_all x3, waiting for transfers between devices, body(): context = lax.all_to_all(context, 'seq', 0, 0, tiled=True)  11 us
  transfers between devices with their start and end apart: 21, of which 8 were waited for; matrix products, arithmetic and copies ran while one was open for 8% of the time, Pallas kernels for 42%

profile of v2, /device:TPU:0, one launch (start us, length us, event | category | flops | bytes accessed | tf_op | source)
XLA Modules:
  0.0 279.6 jit_solution(15897005841463996518)
XLA Ops:
  0.0 1.4 pad_maximum_fusion.1
  1.4 3.0 %collective-permute-start.2 = (bf16[3072]{0:T(1024)(128)(2,1)}, bf16[3072]{0:T(1024)(128)(2,1)}, u32[]{:S(2)}, u32[]{:S(2)}) collective-permute-start(bf16[3072]{0:T(1024)(128)(2,1)} %pad_maximum_fusion.1), channel_id=1, source_target_pairs={{0,1},{1,0},{2,3},{3,2},{4,5},{5,4},{6,7},{7,6},{8,9},{9,8},{10,11... | collective-permute-start | bytes 18440 | tf_op jit(solution)/shard_map/ppermute | solution.py:211
  4.4 1.0 slice.54
  5.5 1.8 slice.57
  7.4 2.0 collective-permute-start.7
  9.4 0.9 slice.22
  10.3 0.8 convert_reduce_fusion.4
  11.1 0.7 convert_element_type.107
  11.8 0.6 pad_add_fusion.1.idx_ref
  12.4 0.2 convert_reduce_fusion.2
  12.6 0.3 convert_reduce_fusion
  12.9 4.6 %collective-permute-done.4 = bf16[128,1536]{1,0:T(8,128)(2,1)S(1)} collective-permute-done((bf16[128,1536]{1,0:T(8,128)(2,1)S(1)}, bf16[128,1536]{1,0:T(8,128)(2,1)S(1)}, u32[]{:S(2)}, u32[]{:S(2)}) %collective-permute-start.4) | collective-permute-done | bytes 393248 | tf_op jit(solution)/shard_map/ppermute | solution.py:211
  17.5 0.2 convert_reduce_fusion.5
  17.8 0.8 slice_convert_fusion.1
  18.6 0.4 collective-permute-done.5
  19.0 1.3 fusion.28
  20.3 7.8 %collective-permute-done.7 = bf16[160,1536]{1,0:T(8,128)(2,1)S(1)} collective-permute-done((bf16[160,1536]{1,0:T(8,128)(2,1)}, bf16[160,1536]{1,0:T(8,128)(2,1)S(1)}, u32[]{:S(2)}, u32[]{:S(2)}) %collective-permute-start.7) | collective-permute-done | bytes 491552 | tf_op jit(solution)/shard_map/ppermute | solution.py:211
  28.0 0.2 convert_reduce_fusion.3
  28.4 15.7 %project.4 = (bf16[8,3,128,128]{3,2,1,0:T(8,128)(2,1)}, bf16[8,3,128,128]{3,2,1,0:T(8,128)(2,1)}) custom-call(s32[4]{0:T(128)} %pad_add_fusion.1.idx_ref, bf16[128,1536]{1,0:T(8,128)(2,1)} %get-tuple-element.48.refs_0_, bf16[128,1536]{1,0:T(8,128)(2,1)} %get-tuple-element.47.refs_1_, bf16[3,3072,2048]{2,1,0:T(8,128)(2,1)} %refs_2_.5), custom_call_target="tpu_custom_call" | custom-call | flops 4831838208 | bytes 37748736 | tf_op jit(solution)/shard_map/project/pallas_call | solution.py:60
  44.1 0.5 collective-permute-start.6
  44.7 1.4 fusion.16
  46.1 16.4 %project.5 = (bf16[8,3,160,128]{3,2,1,0:T(8,128)(2,1)}, bf16[8,3,160,128]{3,2,1,0:T(8,128)(2,1)}) custom-call(s32[4]{0:T(128)} %pad_add_fusion.1.idx_ref, bf16[160,1536]{1,0:T(8,128)(2,1)} %get-tuple-element.40.refs_0_, bf16[160,1536]{1,0:T(8,128)(2,1)} %get-tuple-element.39.refs_1_, bf16[3,3072,2048]{2,1,0:T(8,128)(2,1)} %refs_2_.5), custom_call_target="tpu_custom_call" | custom-call | flops 6039797760 | bytes 37748736 | tf_op jit(solution)/shard_map/project/pallas_call | solution.py:60
  62.5 0.3 convert_reduce_fusion.1
  62.8 0.6 collective-permute-start.1
  63.4 2.5 fusion.35
  65.9 5.8 %all-to-all-start.1 = ((bf16[8,1,3,128,128]{4,3,2,1,0:T(8,128)(2,1)}), bf16[8,1,3,128,128]{4,3,2,1,0:T(8,128)(2,1)}, u32[]{:S(2)}, u32[]{:S(2)}) async-start(bf16[8,1,3,128,128]{4,3,2,1,0:T(8,128)(2,1)} %fusion.35), calls=%async_computation.1 | async-start | bytes 1572864 | tf_op jit(solution)/shard_map/all_to_all | solution.py:268
  71.8 1.8 fusion.4
  73.6 1.2 fusion.23
  74.8 17.5 %all-to-all-done.1.refs_0_.refs_1_.q_ref.refs_2_.refs_5_ = bf16[8,1,3,128,128]{4,3,2,1,0:T(8,128)(2,1)} async-done(((bf16[8,1,3,128,128]{4,3,2,1,0:T(8,128)(2,1)}), bf16[8,1,3,128,128]{4,3,2,1,0:T(8,128)(2,1)}, u32[]{:S(2)}, u32[]{:S(2)}) %all-to-all-start.1) | async-done | bytes 786464 | tf_op jit(solution)/shard_map/all_to_all | solution.py:268
  92.2 4.2 %all-to-all-start.2 = ((bf16[8,1,3,160,128]{4,3,2,1,0:T(8,128)(2,1)}), bf16[8,1,3,160,128]{4,3,2,1,0:T(8,128)(2,1)}, u32[]{:S(2)}, u32[]{:S(2)}) async-start(bf16[8,1,3,160,128]{4,3,2,1,0:T(8,128)(2,1)} %fusion.23), calls=%async_computation.2 | async-start | bytes 1966080 | tf_op jit(solution)/shard_map/all_to_all | solution.py:268
  96.5 18.0 %project.3 = (bf16[8,3,224,128]{3,2,1,0:T(8,128)(2,1)}, bf16[8,3,224,128]{3,2,1,0:T(8,128)(2,1)}) custom-call(s32[4]{0:T(128)} %pad_add_fusion.1.idx_ref, bf16[224,1536]{1,0:T(8,128)(2,1)} %get-tuple-element.44.refs_0_, bf16[224,1536]{1,0:T(8,128)(2,1)} %get-tuple-element.43.refs_1_, bf16[3,3072,2048]{2,1,0:T(8,128)(2,1)} %refs_2_.5), custom_call_target="tpu_custom_call" | custom-call | flops 8455716864 | bytes 37748736 | tf_op jit(solution)/shard_map/project/pallas_call | solution.py:60
  114.5 3.3 %collective-permute-done.3 = bf16[8,3,224,128]{3,2,1,0:T(8,128)(2,1)S(1)} collective-permute-done((bf16[8,3,224,128]{3,2,1,0:T(8,128)(2,1)}, bf16[8,3,224,128]{3,2,1,0:T(8,128)(2,1)S(1)}, u32[]{:S(2)}, u32[]{:S(2)}) %collective-permute-start.3) | collective-permute-done | bytes 1376288 | tf_op jit(solution)/shard_map/ppermute | solution.py:211
  117.9 1.8 fusion.11
  119.6 1.0 all-to-all-done.2.refs_1_.refs_3_.q_ref.refs_4_
  120.7 38.5 %all_to_all.30.q_ref.refs_0_.refs_2_.refs_3_ = bf16[8,1,3,224,128]{4,3,2,1,0:T(8,128)(2,1)} all-to-all(bf16[8,1,3,224,128]{4,3,2,1,0:T(8,128)(2,1)S(1)} %fusion.11), channel_id=1, replica_groups=mesh['seq'=8,'row'=2,'col'=2] {'seq'}, dimensions={0} | all-to-all | bytes 2752512 | tf_op jit(solution)/shard_map/all_to_all | solution.py:268
  159.1 8.7 %attend.9 = bf16[8,1,128,128]{3,2,1,0:T(8,128)(2,1)} custom-call(bf16[8,1,3,128,128]{4,3,2,1,0:T(8,128)(2,1)} %all-to-all-done.1.refs_0_.refs_1_.q_ref.refs_2_.refs_5_, bf16[8,1,3,224,128]{4,3,2,1,0:T(8,128)(2,1)} %all_to_all.30.q_ref.refs_0_.refs_2_.refs_3_, bf16[8,1,3,160,128]{4,3,2,1,0:T(8,128)(2,1)} %all-to-all-done.2.refs_1_.refs_3_.q_ref.refs_4_, ...), custom_call_target="tpu_custom_call" | custom-call | flops 4294967296 | bytes 2621440 | tf_op jit(solution)/shard_map/attend/pallas_call | solution.py:139
  167.9 3.4 %all-to-all-start.5 = ((bf16[8,1,128,128]{3,2,1,0:T(8,128)(2,1)}), bf16[8,1,128,128]{3,2,1,0:T(8,128)(2,1)S(1)}, u32[]{:S(2)}, u32[]{:S(2)}) async-start(bf16[8,1,128,128]{3,2,1,0:T(8,128)(2,1)} %attend.9), calls=%async_computation.5 | async-start | bytes 524288 | tf_op jit(solution)/shard_map/all_to_all | solution.py:290
  171.3 9.2 %attend.7 = (f32[8,1,160,256]{3,2,1,0:T(8,128)}, f32[8,1,160,128]{3,2,1,0:T(8,128)}) custom-call(bf16[8,1,3,160,128]{4,3,2,1,0:T(8,128)(2,1)} %all-to-all-done.2.refs_1_.refs_3_.q_ref.refs_4_, bf16[8,1,3,224,128]{4,3,2,1,0:T(8,128)(2,1)} %all_to_all.30.q_ref.refs_0_.refs_2_.refs_3_, ...), custom_call_target="tpu_custom_call" | custom-call | flops 4026531840 | bytes 2228224 | tf_op jit(solution)/shard_map/attend/pallas_call | solution.py:139
  180.5 6.1 %attend.8 = bf16[8,1,160,128]{3,2,1,0:T(8,128)(2,1)} custom-call(bf16[8,1,3,160,128]{4,3,2,1,0:T(8,128)(2,1)} %all-to-all-done.2.refs_1_.refs_3_.q_ref.refs_4_, bf16[8,1,3,128,128]{4,3,2,1,0:T(8,128)(2,1)} %all-to-all-done.1.refs_0_.refs_1_.q_ref.refs_2_.refs_5_, bf16[8,1,3,128,128]{4,3,2,1,0:T(8,128)(2,1)} %all-to-all-done.1.refs_0_.refs_1_.q_ref.refs_2_.refs_5_, ...), custom_call_target="tpu_custom_call" | custom-call | flops 1342177280 | bytes 1179648 | tf_op jit(solution)/shard_map/attend/pallas_call | solution.py:139
  186.6 5.9 %all-to-all-start.4 = ((bf16[8,1,160,128]{3,2,1,0:T(8,128)(2,1)}), bf16[8,1,160,128]{3,2,1,0:T(8,128)(2,1)S(1)}, u32[]{:S(2)}, u32[]{:S(2)}) async-start(bf16[8,1,160,128]{3,2,1,0:T(8,128)(2,1)} %attend.8), calls=%async_computation.4 | async-start | bytes 655360 | tf_op jit(solution)/shard_map/all_to_all | solution.py:290
  192.5 11.5 %attend.5 = (f32[8,1,224,256]{3,2,1,0:T(8,128)}, f32[8,1,224,128]{3,2,1,0:T(8,128)}) custom-call(bf16[8,1,3,224,128]{4,3,2,1,0:T(8,128)(2,1)} %all_to_all.30.q_ref.refs_0_.refs_2_.refs_3_, bf16[8,1,3,224,128]{4,3,2,1,0:T(8,128)(2,1)} %all_to_all.30.q_ref.refs_0_.refs_2_.refs_3_, bf16[8,1,3,160,128]{4,3,2,1,0:T(8,128)(2,1)} %all-to-all-done.2.refs_1_.refs_3_.q_ref.refs_4_, ...), custom_call_target="tpu_custom_call" | custom-call | flops 5637144576 | bytes 2490368 | tf_op jit(solution)/shard_map/attend/pallas_call | solution.py:139
  204.1 7.6 %attend.6 = bf16[8,1,224,128]{3,2,1,0:T(8,128)(2,1)} custom-call(bf16[8,1,3,224,128]{4,3,2,1,0:T(8,128)(2,1)} %all_to_all.30.q_ref.refs_0_.refs_2_.refs_3_, bf16[8,1,3,128,128]{4,3,2,1,0:T(8,128)(2,1)} %all-to-all-done.1.refs_0_.refs_1_.q_ref.refs_2_.refs_5_, bf16[8,1,3,128,128]{4,3,2,1,0:T(8,128)(2,1)} %all-to-all-done.1.refs_0_.refs_1_.q_ref.refs_2_.refs_5_, ...), custom_call_target="tpu_custom_call" | custom-call | flops 1879048192 | bytes 1441792 | tf_op jit(solution)/shard_map/attend/pallas_call | solution.py:139
  211.7 6.0 %all-to-all-start.3 = ((bf16[8,1,224,128]{3,2,1,0:T(8,128)(2,1)}), bf16[8,1,224,128]{3,2,1,0:T(8,128)(2,1)S(1)}, u32[]{:S(2)}, u32[]{:S(2)}) async-start(bf16[8,1,224,128]{3,2,1,0:T(8,128)(2,1)} %attend.6), calls=%async_computation.3 | async-start | bytes 917504 | tf_op jit(solution)/shard_map/all_to_all | solution.py:290
  217.7 0.5 collective-permute-start.12
  218.2 11.0 %all-to-all-done.3 = bf16[8,1,224,128]{3,2,1,0:T(8,128)(2,1)S(1)} async-done(((bf16[8,1,224,128]{3,2,1,0:T(8,128)(2,1)}), bf16[8,1,224,128]{3,2,1,0:T(8,128)(2,1)S(1)}, u32[]{:S(2)}, u32[]{:S(2)}) %all-to-all-start.3) | async-done | bytes 458784 | tf_op jit(solution)/shard_map/all_to_all | solution.py:290
  229.2 0.7 pad_add_fusion.2.idx_ref
  229.9 0.6 pad_add_fusion.idx_ref
  230.6 0.7 copy-done.9
  231.3 5.0 %output_part.11 = bf16[128,1536]{1,0:T(8,128)(2,1)} custom-call(s32[2]{0:T(128)} %pad_add_fusion.2.idx_ref, bf16[8,128,128]{2,1,0:T(8,128)(2,1)} %bitcast.42, bf16[8,128,128]{2,1,0:T(8,128)(2,1)} %copy-done.9, bf16[2048,3072]{1,0:T(8,128)(2,1)} %w_ref.11), custom_call_target="tpu_custom_call" | custom-call | flops 805306368 | bytes 7077888 | tf_op jit(solution)/shard_map/output_part/pallas_call | solution.py:187
  236.2 0.6 collective-permute-start.15
  236.8 5.0 %output_part.10 = f32[128,1536]{1,0:T(8,128)} custom-call(s32[2]{0:T(128)} %pad_add_fusion.idx_ref, bf16[8,128,128]{2,1,0:T(8,128)(2,1)} %bitcast.43, bf16[8,128,128]{2,1,0:T(8,128)(2,1)} %copy-done.9, bf16[2048,3072]{1,0:T(8,128)(2,1)} %w_ref.11), custom_call_target="tpu_custom_call" | custom-call | flops 805306368 | bytes 7077888 | tf_op jit(solution)/shard_map/output_part/pallas_call | solution.py:187
  241.9 0.7 copy-done.8
  242.6 5.1 %output_part.9 = bf16[160,1536]{1,0:T(8,128)(2,1)} custom-call(s32[2]{0:T(128)} %pad_add_fusion.2.idx_ref, bf16[8,160,128]{2,1,0:T(8,128)(2,1)} %bitcast.39, bf16[8,160,128]{2,1,0:T(8,128)(2,1)} %copy-done.8, bf16[2048,3072]{1,0:T(8,128)(2,1)} %w_ref.11), custom_call_target="tpu_custom_call" | custom-call | flops 1006632960 | bytes 7274496 | tf_op jit(solution)/shard_map/output_part/pallas_call | solution.py:187
  247.7 1.5 collective-permute-start.13
  249.2 5.2 %output_part.8 = f32[160,1536]{1,0:T(8,128)} custom-call(s32[2]{0:T(128)} %pad_add_fusion.idx_ref, bf16[8,160,128]{2,1,0:T(8,128)(2,1)} %bitcast.40, bf16[8,160,128]{2,1,0:T(8,128)(2,1)} %copy-done.8, bf16[2048,3072]{1,0:T(8,128)(2,1)} %w_ref.11), custom_call_target="tpu_custom_call" | custom-call | flops 1006632960 | bytes 7274496 | tf_op jit(solution)/shard_map/output_part/pallas_call | solution.py:187
  254.5 0.8 copy-done.7
  255.2 5.4 %output_part.7 = bf16[224,1536]{1,0:T(8,128)(2,1)} custom-call(s32[2]{0:T(128)} %pad_add_fusion.2.idx_ref, bf16[8,224,128]{2,1,0:T(8,128)(2,1)} %bitcast.36, bf16[8,224,128]{2,1,0:T(8,128)(2,1)} %copy-done.7, bf16[2048,3072]{1,0:T(8,128)(2,1)} %w_ref.11), custom_call_target="tpu_custom_call" | custom-call | flops 1409286144 | bytes 7667712 | tf_op jit(solution)/shard_map/output_part/pallas_call | solution.py:187
  260.7 0.5 collective-permute-start.11
  261.2 1.1 fusion.34
  262.3 5.7 %output_part.6 = f32[224,1536]{1,0:T(8,128)} custom-call(s32[2]{0:T(128)} %pad_add_fusion.idx_ref, bf16[8,224,128]{2,1,0:T(8,128)(2,1)} %bitcast.37, bf16[8,224,128]{2,1,0:T(8,128)(2,1)} %copy-done.7, bf16[2048,3072]{1,0:T(8,128)(2,1)} %w_ref.11), custom_call_target="tpu_custom_call" | custom-call | flops 1409286144 | bytes 7667712 | tf_op jit(solution)/shard_map/output_part/pallas_call | solution.py:187
  268.0 1.3 fusion.22
  269.3 8.8 %collective-permute-done.11 = bf16[224,1536]{1,0:T(8,128)(2,1)S(1)} collective-permute-done((bf16[224,1536]{1,0:T(8,128)(2,1)}, bf16[224,1536]{1,0:T(8,128)(2,1)S(1)}, u32[]{:S(2)}, u32[]{:S(2)}) %collective-permute-start.11) | collective-permute-done | bytes 688160 | tf_op jit(solution)/shard_map/ppermute | solution.py:211
  278.1 0.3 fusion.10
  278.4 1.2 pad_maximum_fusion
  (64 shorter events, 0.5 us)
Async XLA Ops:
  0.0 9.4 %copy-start = (bf16[512,1536]{1,0:T(8,128)(2,1)S(1)}, bf16[512,1536]{1,0:T(8,128)(2,1)}, u32[]{:S(2)}) copy-start(bf16[512,1536]{1,0:T(8,128)(2,1)} %param.5) | copy-start | bytes 4718596
  1.4 16.4 %collective-permute-start.2 = (bf16[3072]{0:T(1024)(128)(2,1)}, bf16[3072]{0:T(1024)(128)(2,1)}, u32[]{:S(2)}, u32[]{:S(2)}) collective-permute-start(bf16[3072]{0:T(1024)(128)(2,1)} %pad_maximum_fusion.1), channel_id=1, source_target_pairs={{0,1},{1,0},{2,3},{3,2},{4,5},{5,4},{6,7},{7,6},{8,9},{9,8},{10,11... | collective-permute-start | bytes 18440 | tf_op jit(solution)/shard_map/ppermute | solution.py:211
  5.4 5.6 %copy-start.11 = (bf16[1536]{0:T(1024)(128)(2,1)S(1)}, bf16[1536]{0:T(1024)(128)(2,1)}, u32[]{:S(2)}) copy-start(bf16[1536]{0:T(1024)(128)(2,1)} %param.6) | copy-start | bytes 9220
  5.5 12.1 %collective-permute-start.4 = (bf16[128,1536]{1,0:T(8,128)(2,1)S(1)}, bf16[128,1536]{1,0:T(8,128)(2,1)S(1)}, u32[]{:S(2)}, u32[]{:S(2)}) collective-permute-start(bf16[128,1536]{1,0:T(8,128)(2,1)S(1)} %slice.54), channel_id=1, source_target_pairs={{0,1},{1,0},{2,3},{3,2},{4,5},{5,4},{6,7},{7,6},{8,9},{9,8},{10,11... | collective-permute-start | bytes 1179656 | tf_op jit(solution)/shard_map/ppermute | solution.py:211
  7.4 20.7 %collective-permute-start.7 = (bf16[160,1536]{1,0:T(8,128)(2,1)}, bf16[160,1536]{1,0:T(8,128)(2,1)S(1)}, u32[]{:S(2)}, u32[]{:S(2)}) collective-permute-start(bf16[160,1536]{1,0:T(8,128)(2,1)} %slice.57), channel_id=1, source_target_pairs={{0,1},{1,0},{2,3},{3,2},{4,5},{5,4},{6,7},{7,6},{8,9},{9,8},{10,11... | collective-permute-start | bytes 1474568 | tf_op jit(solution)/shard_map/ppermute | solution.py:211
  10.3 52.2 %collective-permute-start = (bf16[224,1536]{1,0:T(8,128)(2,1)}, bf16[224,1536]{1,0:T(8,128)(2,1)S(1)}, u32[]{:S(2)}, u32[]{:S(2)}) collective-permute-start(bf16[224,1536]{1,0:T(8,128)(2,1)} %slice.22), channel_id=1, source_target_pairs={{0,1},{1,0},{2,3},{3,2},{4,5},{5,4},{6,7},{7,6},{8,9},{9,8},{10,11... | collective-permute-start | bytes 2064392 | tf_op jit(solution)/shard_map/ppermute | solution.py:211
  11.8 5.9 %copy-start.12 = (f32[128]{0:T(128)S(1)}, f32[128]{0:T(128)}, u32[]{:S(2)}) copy-start(f32[128]{0:T(128)} %get-tuple-element.29) | copy-start | bytes 1540
  11.8 5.9 %copy-start.13 = (f32[128]{0:T(128)S(1)}, f32[128]{0:T(128)}, u32[]{:S(2)}) copy-start(f32[128]{0:T(128)} %get-tuple-element.30) | copy-start | bytes 1540
  17.7 1.2 collective-permute-start.5
  28.3 16.3 %collective-permute-start.8 = (f32[2,160]{1,0:T(2,128)S(1)}, f32[2,160]{1,0:T(2,128)S(1)}, u32[]{:S(2)}, u32[]{:S(2)}) collective-permute-start(f32[2,160]{1,0:T(2,128)S(1)} %pad_maximum_fusion.3), channel_id=1, source_target_pairs={{0,2},{2,0},{1,3},{3,1},{4,6},{6,4},{5,7},{7,5},{8,10},{10,8},{9,1... | collective-permute-start | bytes 3848 | tf_op jit(solution)/shard_map/ppermute | solution.py:211
  44.1 19.3 %collective-permute-start.6 = (bf16[8,3,128,128]{3,2,1,0:T(8,128)(2,1)}, bf16[8,3,128,128]{3,2,1,0:T(8,128)(2,1)}, u32[]{:S(2)}, u32[]{:S(2)}) collective-permute-start(bf16[8,3,128,128]{3,2,1,0:T(8,128)(2,1)} %get-tuple-element.18), channel_id=1, source_target_pairs={{0,2},{2,0},{1,3},{3,1},{4,6},{6,4},{5,7},{7,5},{8,10},{10,8},{9,1... | collective-permute-start | bytes 2359304 | tf_op jit(solution)/shard_map/ppermute | solution.py:211
  62.5 11.1 %collective-permute-start.9 = (bf16[8,3,160,128]{3,2,1,0:T(8,128)(2,1)}, bf16[8,3,160,128]{3,2,1,0:T(8,128)(2,1)S(1)}, u32[]{:S(2)}, u32[]{:S(2)}) collective-permute-start(bf16[8,3,160,128]{3,2,1,0:T(8,128)(2,1)} %get-tuple-element.20), channel_id=1, source_target_pairs={{0,2},{2,0},{1,3},{3,1},{4,6},{6,4},{5,7},{7,5},{8,10},{10,8},{9,1... | collective-permute-start | bytes 2949128 | tf_op jit(solution)/shard_map/ppermute | solution.py:211
  62.8 8.9 %collective-permute-start.1 = (f32[2,224]{1,0:T(2,128)S(1)}, f32[2,224]{1,0:T(2,128)S(1)}, u32[]{:S(2)}, u32[]{:S(2)}) collective-permute-start(f32[2,224]{1,0:T(2,128)S(1)} %pad_maximum_fusion.2), channel_id=1, source_target_pairs={{0,2},{2,0},{1,3},{3,1},{4,6},{6,4},{5,7},{7,5},{8,10},{10,8},{9,1... | collective-permute-start | bytes 5384 | tf_op jit(solution)/shard_map/ppermute | solution.py:211
  65.9 26.3 %all-to-all-start.1 = ((bf16[8,1,3,128,128]{4,3,2,1,0:T(8,128)(2,1)}), bf16[8,1,3,128,128]{4,3,2,1,0:T(8,128)(2,1)}, u32[]{:S(2)}, u32[]{:S(2)}) async-start(bf16[8,1,3,128,128]{4,3,2,1,0:T(8,128)(2,1)} %fusion.35), calls=%async_computation.1 | async-start | bytes 1572864 | tf_op jit(solution)/shard_map/all_to_all | solution.py:268
  71.8 1.8 copy-start.10
  92.2 28.4 %all-to-all-start.2 = ((bf16[8,1,3,160,128]{4,3,2,1,0:T(8,128)(2,1)}), bf16[8,1,3,160,128]{4,3,2,1,0:T(8,128)(2,1)}, u32[]{:S(2)}, u32[]{:S(2)}) async-start(bf16[8,1,3,160,128]{4,3,2,1,0:T(8,128)(2,1)} %fusion.23), calls=%async_computation.2 | async-start | bytes 1966080 | tf_op jit(solution)/shard_map/all_to_all | solution.py:268
  114.5 3.3 %collective-permute-start.3 = (bf16[8,3,224,128]{3,2,1,0:T(8,128)(2,1)}, bf16[8,3,224,128]{3,2,1,0:T(8,128)(2,1)S(1)}, u32[]{:S(2)}, u32[]{:S(2)}) collective-permute-start(bf16[8,3,224,128]{3,2,1,0:T(8,128)(2,1)} %get-tuple-element.16), channel_id=1, source_target_pairs={{0,2},{2,0},{1,3},{3,1},{4,6},{6,4},{5,7},{7,5},{8,10},{10,8},{9,1... | collective-permute-start | bytes 4128776 | tf_op jit(solution)/shard_map/ppermute | solution.py:211
  167.9 18.7 %all-to-all-start.5 = ((bf16[8,1,128,128]{3,2,1,0:T(8,128)(2,1)}), bf16[8,1,128,128]{3,2,1,0:T(8,128)(2,1)S(1)}, u32[]{:S(2)}, u32[]{:S(2)}) async-start(bf16[8,1,128,128]{3,2,1,0:T(8,128)(2,1)} %attend.9), calls=%async_computation.5 | async-start | bytes 524288 | tf_op jit(solution)/shard_map/all_to_all | solution.py:290
  186.6 31.1 %copy-start.6 = (bf16[8,1,128,128]{3,2,1,0:T(8,128)(2,1)}, bf16[8,1,128,128]{3,2,1,0:T(8,128)(2,1)S(1)}, u32[]{:S(2)}) copy-start(bf16[8,1,128,128]{3,2,1,0:T(8,128)(2,1)S(1)} %all-to-all-done.5) | copy-start | bytes 786436
  186.6 25.1 %all-to-all-start.4 = ((bf16[8,1,160,128]{3,2,1,0:T(8,128)(2,1)}), bf16[8,1,160,128]{3,2,1,0:T(8,128)(2,1)S(1)}, u32[]{:S(2)}, u32[]{:S(2)}) async-start(bf16[8,1,160,128]{3,2,1,0:T(8,128)(2,1)} %attend.8), calls=%async_computation.4 | async-start | bytes 655360 | tf_op jit(solution)/shard_map/all_to_all | solution.py:290
  211.7 24.6 %copy-start.5 = (bf16[8,1,160,128]{3,2,1,0:T(8,128)(2,1)}, bf16[8,1,160,128]{3,2,1,0:T(8,128)(2,1)S(1)}, u32[]{:S(2)}) copy-start(bf16[8,1,160,128]{3,2,1,0:T(8,128)(2,1)S(1)} %all-to-all-done.4) | copy-start | bytes 983044
  211.7 17.5 %all-to-all-start.3 = ((bf16[8,1,224,128]{3,2,1,0:T(8,128)(2,1)}), bf16[8,1,224,128]{3,2,1,0:T(8,128)(2,1)S(1)}, u32[]{:S(2)}, u32[]{:S(2)}) async-start(bf16[8,1,224,128]{3,2,1,0:T(8,128)(2,1)} %attend.6), calls=%async_computation.3 | async-start | bytes 917504 | tf_op jit(solution)/shard_map/all_to_all | solution.py:290
  217.7 12.9 %collective-permute-start.14 = (bf16[8,128,128]{2,1,0:T(8,128)(2,1)S(1)}, bf16[8,128,128]{2,1,0:T(8,128)(2,1)S(1)}, u32[]{:S(2)}, u32[]{:S(2)}) collective-permute-start(bf16[8,128,128]{2,1,0:T(8,128)(2,1)S(1)} %bitcast.41), channel_id=1, source_target_pairs={{0,2},{2,0},{1,3},{3,1},{4,6},{6,4},{5,7},{7,5},{8,10},{10,8},{9,1... | collective-permute-start | bytes 786440 | tf_op jit(solution)/shard_map/ppermute | solution.py:211
  217.7 24.1 %collective-permute-start.12 = (bf16[8,160,128]{2,1,0:T(8,128)(2,1)S(1)}, bf16[8,160,128]{2,1,0:T(8,128)(2,1)S(1)}, u32[]{:S(2)}, u32[]{:S(2)}) collective-permute-start(bf16[8,160,128]{2,1,0:T(8,128)(2,1)S(1)} %bitcast.38), channel_id=1, source_target_pairs={{0,2},{2,0},{1,3},{3,1},{4,6},{6,4},{5,7},{7,5},{8,10},{10,8},{9,1... | collective-permute-start | bytes 983048 | tf_op jit(solution)/shard_map/ppermute | solution.py:211
  229.2 7.1 %copy-start.2 = (bf16[8,1,224,128]{3,2,1,0:T(8,128)(2,1)}, bf16[8,1,224,128]{3,2,1,0:T(8,128)(2,1)S(1)}, u32[]{:S(2)}) copy-start(bf16[8,1,224,128]{3,2,1,0:T(8,128)(2,1)S(1)} %all-to-all-done.3) | copy-start | bytes 1376260
  229.2 25.3 %collective-permute-start.10 = (bf16[8,224,128]{2,1,0:T(8,128)(2,1)S(1)}, bf16[8,224,128]{2,1,0:T(8,128)(2,1)S(1)}, u32[]{:S(2)}, u32[]{:S(2)}) collective-permute-start(bf16[8,224,128]{2,1,0:T(8,128)(2,1)S(1)} %bitcast.35), channel_id=1, source_target_pairs={{0,2},{2,0},{1,3},{3,1},{4,6},{6,4},{5,7},{7,5},{8,10},{10,8},{9,1... | collective-permute-start | bytes 1376264 | tf_op jit(solution)/shard_map/ppermute | solution.py:211
  230.6 0.7 copy-start.9
  236.2 24.9 %collective-permute-start.15 = (bf16[128,1536]{1,0:T(8,128)(2,1)}, bf16[128,1536]{1,0:T(8,128)(2,1)}, u32[]{:S(2)}, u32[]{:S(2)}) collective-permute-start(bf16[128,1536]{1,0:T(8,128)(2,1)} %output_part.11), channel_id=1, source_target_pairs={{0,1},{1,0},{2,3},{3,2},{4,5},{5,4},{6,7},{7,6},{8,9},{9,8},{10,11... | collective-permute-start | bytes 1179656 | tf_op jit(solution)/shard_map/ppermute | solution.py:211
  241.9 0.7 copy-start.8
  247.7 20.3 %collective-permute-start.13 = (bf16[160,1536]{1,0:T(8,128)(2,1)}, bf16[160,1536]{1,0:T(8,128)(2,1)}, u32[]{:S(2)}, u32[]{:S(2)}) collective-permute-start(bf16[160,1536]{1,0:T(8,128)(2,1)} %output_part.9), channel_id=1, source_target_pairs={{0,1},{1,0},{2,3},{3,2},{4,5},{5,4},{6,7},{7,6},{8,9},{9,8},{10,11... | collective-permute-start | bytes 1474568 | tf_op jit(solution)/shard_map/ppermute | solution.py:211
  254.5 6.7 %copy-start.4 = (f32[128,1536]{1,0:T(8,128)S(1)}, f32[128,1536]{1,0:T(8,128)}, u32[]{:S(2)}) copy-start(f32[128,1536]{1,0:T(8,128)} %output_part.10) | copy-start | bytes 2359300
  254.5 0.8 copy-start.7
  260.7 17.4 %collective-permute-start.11 = (bf16[224,1536]{1,0:T(8,128)(2,1)}, bf16[224,1536]{1,0:T(8,128)(2,1)S(1)}, u32[]{:S(2)}, u32[]{:S(2)}) collective-permute-start(bf16[224,1536]{1,0:T(8,128)(2,1)} %output_part.7), channel_id=1, source_target_pairs={{0,1},{1,0},{2,3},{3,2},{4,5},{5,4},{6,7},{7,6},{8,9},{9,8},{10,11... | collective-permute-start | bytes 2064392 | tf_op jit(solution)/shard_map/ppermute | solution.py:211
  262.3 5.7 %copy-start.3 = (f32[160,1536]{1,0:T(8,128)S(1)}, f32[160,1536]{1,0:T(8,128)}, u32[]{:S(2)}) copy-start(f32[160,1536]{1,0:T(8,128)} %output_part.8) | copy-start | bytes 2949124
  268.0 10.1 %copy-start.1 = (f32[224,1536]{1,0:T(8,128)S(1)}, f32[224,1536]{1,0:T(8,128)}, u32[]{:S(2)}) copy-start(f32[224,1536]{1,0:T(8,128)} %output_part.6) | copy-start | bytes 4128772
